TPU v7x, 32 devices: a whole 2x2x4 slice. The times are simulated.
32 devices in a mesh: row: 4 (over x, core), col: 8 (over z, y).
Axes of the slice: x: 2, y: 2, z: 4, core: 2. Of those that a mesh axis runs over, the one named last changes fastest.
Arguments:
- forcing: float32 [2, 1024, 2048], P(None, 'row', 'col'), may hold values from -6 to 6
- wave_index: int32 [1], replicated, may hold values from 12 to 27
- directions: int32 [32], replicated, may hold values from 0 to 63
- row_coupling: float32 [4, 4], replicated, may hold values from -1 to 2, as said below
- col_coupling: float32 [8, 8], replicated, may hold values from -1 to 2, as said below
- mode_coupling: float32 [256, 256], replicated, may hold values from -1 to 2, as said below
Outputs:
- field: float32 [2, 1024, 2048], P(None, 'row', 'col')
Inputs may be any that keep to these rules, and one draw needn't show every extreme that they name: `row_coupling`: entries of a coarse correction factor. `col_coupling`: entries of a coarse correction factor. `mode_coupling`: entries of a coarse correction factor.
All inputs are finite; a program needn't handle non-finite values.
Results may differ from a plain program's by a relative error of at most 0.0003.
Values sent between devices are 32-bit elements; how exact they have to be, the bound alone decides.
No kernel may reach another device: no remote copies, remote signals or barrier semaphores. Data moves between devices by JAX's collectives and lax.ppermute only.
A program may use at most 64 MiB of HBM per device.

v0:
```python
import functools
import math

import jax
import jax.numpy as jnp
import numpy as np
from jax import lax
from jax.experimental import pallas as pl
from jax.experimental.pallas import tpu as pltpu
from jax.sharding import PartitionSpec as P

ANGLES = 64
KAPPA_UNIT = 0.04
DAMPING = 0.5
F32 = jnp.float32
BF16 = jnp.bfloat16
NN = (((1,), (0,)), ((), ()))
NT = (((1,), (1,)), ((), ()))
TN = (((0,), (0,)), ((), ()))
VMEM = pl.BlockSpec(memory_space=pltpu.VMEM)
SMEM = pl.BlockSpec(memory_space=pltpu.SMEM)


def split(a):
    if isinstance(a, tuple):
        return a
    high = a.astype(BF16)
    return high, (a - high.astype(F32)).astype(BF16)


def dot(a, b, dims=NN):
    ah, al = split(a)
    bh, bl = split(b)
    mul = functools.partial(lax.dot_general, dimension_numbers=dims, preferred_element_type=F32)
    return mul(ah, bh) + (mul(ah, bl) + mul(al, bh))


def cmul(a, b):
    return a[0] * b[0] - a[1] * b[1], a[0] * b[1] + a[1] * b[0]


def add(*terms):
    return sum(t[0] for t in terms[1:]) + terms[0][0], sum(t[1] for t in terms[1:]) + terms[0][1]


def sub(a, b):
    return a[0] - b[0], a[1] - b[1]


def sine_table(width):
    index = np.arange(1, width + 1)
    basis = np.sqrt(2.0 / (width + 1)) * np.sin(np.pi / (width + 1) * (np.outer(index, index) % (2 * width + 2)))
    values = 2.0 - 2.0 * np.cos(np.pi / (width + 1) * index)
    return basis.astype(np.float32), values.astype(np.float32)


def lanes(shape):
    return lax.broadcasted_iota(jnp.int32, shape, len(shape) - 1)


def parity(width):
    return (1 - 2 * (lanes((1, width)) & 1)).astype(F32)


def inverse_symbol(col_values, row_values, kappa):
    shift = kappa * kappa
    real = col_values + row_values - shift
    imag = DAMPING * shift
    norm = 1.0 / (real * real + imag * imag)
    return real * norm, imag * norm


def turn(z, half):
    sign = jnp.where(lanes((1, 2 * half)) < half, -1.0, 1.0)
    return sign * pltpu.roll(z, half, 1)


def contract(rows, table):
    count, half = rows[0].shape[0], table[0].shape[0] // 2
    out = dot(jnp.concatenate(rows, 0), table, NT)
    return out[:count] + turn(out[count:], half)


def first_kernel(wave, forcing, qh, ql, rows, lam_col, dirs, payload, spectrum, hat, along, *, width, modes, count):
    kappa = KAPPA_UNIT * wave[0].astype(F32)
    basis = (qh[...], ql[...])
    line = lanes((1, width)).astype(F32)
    ramp = (line + 0.5) / width
    windows = (1.0 - ramp, ramp)
    theta = 2.0 * math.pi / ANGLES * dirs[...]
    tables = []
    for speed in (jnp.cos(theta), jnp.sin(theta)):
        phase = kappa * speed[:, :1] * line
        cosine, sine = jnp.cos(phase), jnp.sin(phase)
        tables += [w * cosine for w in windows] + [-w * sine for w in windows]
    table = jnp.concatenate(tables, 0)
    along[...] = table[4 * modes :]
    hats = dot(table, basis)
    hat[...] = hats
    across_hat, along_hat = split(hats[: 4 * modes]), split(hats[4 * modes :])

    half_way = dot(forcing[...].reshape(2 * width, width), basis)
    coeff = [dot(basis, half_way[:width]), dot(basis, half_way[width:])]
    spectrum[0] = coeff[0]
    spectrum[1] = coeff[1]
    inv = inverse_symbol(lam_col[...], rows[4:5], kappa)
    coeff = [split(c) for c in cmul(coeff, inv)]
    weights = split(rows[...])
    out = []
    vectors = []
    for dims, table_hat in ((NN, along_hat), (NT, across_hat)):
        real, imag = dot(weights, coeff[0], dims), dot(weights, coeff[1], dims)
        edges = []
        for near, inner in ((0, 1), (2, 3)):
            e = real[near : near + 1], imag[near : near + 1]
            d = sub(e, (real[inner : inner + 1], imag[inner : inner + 1]))
            edges.append(e)
            vectors += [e[0] - kappa * d[1], e[1] + kappa * d[0]]
        rows_r = jnp.concatenate([edges[0][0], edges[1][0]] + [edges[0][0]] * 6, 0)
        rows_i = jnp.concatenate([edges[0][1], edges[1][1]] + [edges[0][1]] * 6, 0)
        proj = contract((rows_r, rows_i), table_hat)
        out += [proj[0:1], proj[1:2]]
    flat = jnp.concatenate(out + vectors, 1)
    payload[...] = jnp.broadcast_to(flat, payload.shape)


def second_kernel(
    wave, own, gathered, spectrum, hat, along, coupling, mode, qh, ql, rows, lam_col, dirs_row, field, *, width, modes, nb
):
    count = gathered.shape[0]
    kappa = KAPPA_UNIT * wave[0].astype(F32)
    unknowns = 8 * modes
    half = 2 * modes
    inv = inverse_symbol(lam_col[...], rows[4:5], kappa)
    inv_split = split(inv[0]), split(inv[1])
    sign = parity(width)
    q0, q1 = rows[0:1], rows[1:2]
    robin_weight = q0, kappa * (q0 - q1)
    diag_rows = split(jnp.concatenate([q0 * q0, sign * q0 * q0, q0 * (q0 - q1), sign * q0 * (q0 - q1)] * 2, 0))
    diag = dot(diag_rows, inv_split[0]), dot(diag_rows, inv_split[1])
    same = diag[0][0:1], diag[1][0:1]
    opposite = diag[0][1:2], diag[1][1:2]
    same_robin = diag[0][0:1] - kappa * diag[1][2:3], diag[1][0:1] + kappa * diag[0][2:3]
    opposite_robin = diag[0][1:2] - kappa * diag[1][3:4], diag[1][1:2] + kappa * diag[0][3:4]
    hats = hat[...]
    across_hat, along_hat = split(hats[: 2 * half]), split(hats[2 * half :])
    tables = {"t": along_hat, "b": along_hat, "l": across_hat, "r": across_hat}
    mode_split = split(mode[...])

    lane = lanes((1, 4 * modes))
    theta = 2.0 * math.pi / ANGLES * dirs_row[...]
    speeds = jnp.cos(theta), jnp.sin(theta)
    pick = lane // half, (lane // modes) % 2

    def wave_at(axis, x):
        ramp = (x + 0.5) / width
        window = jnp.where(pick[axis] == 0, 1.0 - ramp, ramp)
        phase = kappa * speeds[axis] * float(x)
        return window * jnp.cos(phase), -window * jnp.sin(phase)

    ends = {}
    for side, axis, near, inner in (("t", 0, 0, 1), ("b", 0, width - 1, width - 2), ("l", 1, 0, 1), ("r", 1, width - 1, width - 2)):
        e, n = wave_at(axis, near), wave_at(axis, inner)
        er, ei, nr, ni = e[0], -e[1], n[0], -n[1]
        ends[side] = e, (er - kappa * (ei - ni), ei + kappa * (er - nr))
    facing = {"t": "b", "b": "t", "l": "r", "r": "l"}

    def spread(proj, side):
        low = lane < half
        if side in "tb":
            real = jnp.where(low, proj, pltpu.roll(proj, half, 1))
            imag = jnp.where(low, pltpu.roll(proj, half, 1), proj)
        else:
            by1, by2, by3 = (pltpu.roll(proj, k * modes, 1) for k in (1, 2, 3))
            block = lane // modes
            real = jnp.where(block == 0, proj, jnp.where(block == 3, by2, by1))
            imag = jnp.where(block == 0, by2, jnp.where(block == 3, proj, by3))
        parts = cmul((real, imag), ends[facing[side]][0])
        return jnp.concatenate(parts, 1)

    def outgoing(c, side):
        z = cmul((c[:, : unknowns // 2], c[:, unknowns // 2 :]), ends[side][1])
        low = lane < half
        if side in "tb":
            z = [a + pltpu.roll(a, half, 1) for a in z]
            z = jnp.where(low, z[0], z[1])
        else:
            z = [a + pltpu.roll(a, 3 * modes, 1) for a in z]
            block = lane // modes
            back = pltpu.roll(z[0], 3 * modes, 1)
            ahead = pltpu.roll(z[1], modes, 1)
            z = jnp.where(
                block == 0, z[0], jnp.where(block == 1, back, jnp.where(block == 2, pltpu.roll(z[1], 2 * modes, 1), ahead))
            )
        return z

    def synth(zs, table):
        size = zs[0].shape[0]
        stacked = jnp.concatenate([a for z in zs for a in (z, -turn(z, half))], 0)
        out = dot(stacked, table)
        return [(out[2 * k * size : (2 * k + 1) * size], out[(2 * k + 1) * size : (2 * k + 2) * size]) for k in range(len(zs))]

    def coarse_of(projs):
        total = 0.0
        for k, side in enumerate("tblr"):
            total = total + dot(coupling[k], spread(projs[side], side))
        return dot(total, mode_split, NT)

    def robin_of(c, base):
        tb = synth([outgoing(c, "t"), outgoing(c, "b")], along_hat)
        lr = synth([outgoing(c, "l"), outgoing(c, "r")], across_hat)
        return {side: add(base[side], s) for side, s in zip("tblr", tb + lr)}

    row = lax.broadcasted_iota(jnp.int32, (count, 1), 0)
    first, last = row % nb == 0, row % nb == nb - 1

    def incoming(out):
        zero = jnp.zeros((nb, width), F32)
        down = lambda a: jnp.concatenate([zero, a[:-nb]], 0)
        up = lambda a: jnp.concatenate([a[nb:], zero], 0)
        right = lambda a: jnp.where(first, 0.0, pltpu.roll(a, 1, 0))
        left = lambda a: jnp.where(last, 0.0, pltpu.roll(a, count - 1, 0))
        move = lambda f, z: (f(z[0]), f(z[1]))
        return {"t": move(down, out["b"]), "b": move(up, out["t"]), "l": move(right, out["r"]), "r": move(left, out["l"])}

    def apply_inverse(vectors):
        size = vectors[0][0].shape[0]
        k = len(vectors)
        stacked = split(jnp.concatenate([v[0] for v in vectors] + [v[1] for v in vectors], 0))
        a, b = dot(stacked, inv_split[0]), dot(stacked, inv_split[1])
        real, imag = a[: k * size] - b[k * size :], a[k * size :] + b[: k * size]
        return [(real[j * size : (j + 1) * size], imag[j * size : (j + 1) * size]) for j in range(k)]

    def scale(r, z):
        return r * z[0], r * z[1]

    def responses(g):
        edge, rob = {}, {}
        for (a, b), (c, d) in ((("t", "b"), ("l", "r")), (("l", "r"), ("t", "b"))):
            vectors = []
            for src in (a, b):
                plain, heavy = scale(q0, g[src]), cmul(g[src], robin_weight)
                vectors += [plain, scale(sign, plain), heavy, scale(sign, heavy)]
            x = apply_inverse(vectors)
            cross = [scale(q0, add(x[k], scale(sign, x[k + 4]))) for k in range(4)]
            edge[c], edge[d], rob[c], rob[d] = cross
        for a, b in (("t", "b"), ("l", "r")):
            edge[a] = add(edge[a], cmul(g[a], same), cmul(g[b], opposite))
            edge[b] = add(edge[b], cmul(g[b], same), cmul(g[a], opposite))
            rob[a] = add(rob[a], cmul(g[a], same_robin), cmul(g[b], opposite_robin))
            rob[b] = add(rob[b], cmul(g[b], same_robin), cmul(g[a], opposite_robin))
        return edge, rob

    values = gathered[...]
    lanes_of = 4 * modes
    proj0 = {s: values[:, k * lanes_of : (k + 1) * lanes_of] for k, s in enumerate("tblr")}
    at = 4 * lanes_of
    robin0 = {}
    for s in "tblr":
        robin0[s] = values[:, at : at + width], values[:, at + width : at + 2 * width]
        at += 2 * width

    out1 = robin_of(coarse_of(proj0), robin0)
    edge, rob = responses(incoming(out1))
    proj1 = {}
    for a, b in (("t", "b"), ("l", "r")):
        ja, jb = sub(edge[a], out1[a]), sub(edge[b], out1[b])
        both = contract((jnp.concatenate([ja[0], jb[0]], 0), jnp.concatenate([ja[1], jb[1]], 0)), tables[a])
        proj1[a], proj1[b] = proj0[a] + both[:count], proj0[b] + both[count:]
    base = {s: add(robin0[s], rob[s]) for s in "tblr"}
    out2 = robin_of(coarse_of(proj1), base)
    g2 = incoming(out2)

    mine = own[0]
    picks = [coupling[k, pl.ds(mine, 1), :] for k in range(4)]
    one = (lanes((1, count)) == mine).astype(F32)
    weights = split(jnp.concatenate(picks + [one] * 4, 0))
    mixed = {s: (dot(weights, g2[s][0]), dot(weights, g2[s][1])) for s in "tblr"}
    sent = {s: (dot(weights, out2[s][0]), dot(weights, out2[s][1])) for s in "tblr"}
    base0 = {s: dot(weights, proj0[s]) for s in "tblr"}
    index = {"t": 0, "b": 1, "l": 2, "r": 3}
    rowof = lambda z, k: (z[0][k : k + 1], z[1][k : k + 1])
    vectors = []
    order = []
    for o in "tblr":
        weight = scale(sign, (q0, q0)) if o in "br" else (q0, q0)
        for src in ("lr" if o in "tb" else "tb"):
            z = rowof(mixed[src], index[o])
            vectors.append((weight[0] * z[0], weight[0] * z[1]))
            order.append((o, src))
    x = apply_inverse(vectors)
    total = jnp.zeros((1, unknowns), F32)
    jumps = {}
    for o in "tblr":
        k = 2 * index[o]
        e = scale(q0, add(x[k], scale(sign, x[k + 1])))
        e = add(e, cmul(rowof(mixed[o], index[o]), same), cmul(rowof(mixed[facing[o]], index[o]), opposite))
        jumps[o] = sub(e, rowof(sent[o], index[o]))
    for a, b in (("t", "b"), ("l", "r")):
        rr = jnp.concatenate([jumps[a][0], jumps[b][0]] + [jumps[a][0]] * 6, 0)
        ri = jnp.concatenate([jumps[a][1], jumps[b][1]] + [jumps[a][1]] * 6, 0)
        both = contract((rr, ri), tables[a])
        for j, o in enumerate((a, b)):
            k = index[o]
            total = total + spread(base0[o][k : k + 1] + both[j : j + 1], o)
    c2 = dot(jnp.broadcast_to(total, (8, unknowns)), mode_split, NT)[0:1]

    mine_g = {s: rowof(mixed[s], 4) for s in "tblr"}
    basis = (qh[...], ql[...])
    coeff = []
    zero = jnp.zeros((4, width), F32)
    sq0 = sign * q0
    for part in range(2):
        left_rows = jnp.concatenate([q0, sq0, mine_g["l"][part], mine_g["r"][part], zero], 0)
        right_rows = jnp.concatenate([mine_g["t"][part], mine_g["b"][part], q0, sq0, zero], 0)
        coeff.append(spectrum[part] + dot(left_rows, right_rows, TN))
    coeff = cmul(coeff, inv)
    half_way = [dot(basis, coeff[0]), dot(basis, coeff[1])]

    cr, ci = c2[:, : 4 * modes], c2[:, 4 * modes :]
    low = lane < half
    flip = lambda a: pltpu.roll(a, half, 1)
    a0, a1 = jnp.where(low, cr, flip(ci)), jnp.where(low, flip(cr), ci)
    line = lax.broadcasted_iota(jnp.int32, (width, 1), 0).astype(F32)
    ramp = (line + 0.5) / width
    phase = kappa * speeds[0] * line
    plain = (1.0 - ramp) * a0 + ramp * a1
    turned = (1.0 - ramp) * turn(a0, half) + ramp * turn(a1, half)
    v = jnp.cos(phase) * plain + jnp.sin(phase) * turned
    along_split = split(along[...])
    field[0] = dot(half_way[0], basis) + dot(v, along_split)
    field[1] = dot(half_way[1], basis) + dot(-turn(v, half), along_split)


def local(forcing, wave_index, directions, row_coupling, col_coupling, mode_coupling):
    width = forcing.shape[1]
    modes = directions.shape[0]
    na, nb = row_coupling.shape[0], col_coupling.shape[0]
    count = na * nb
    size = 4 * 4 * modes + 4 * 2 * width
    basis, values = sine_table(width)
    qh = basis.astype(jnp.bfloat16)
    ql = (basis - qh.astype(np.float32)).astype(jnp.bfloat16)
    sign = 1.0 - 2.0 * (np.arange(width) % 2)
    rows = np.zeros((8, width), np.float32)
    rows[0], rows[1], rows[2], rows[3], rows[4] = basis[0], basis[1], sign * basis[0], sign * basis[1], values
    lam_col = np.ascontiguousarray(values[:, None])
    turns = directions.astype(F32)
    dirs = jnp.broadcast_to(turns[:, None], (modes, 128))
    dirs_row = jnp.tile(turns, 4)[None, :]

    scale = 1.0 / math.sqrt(width) / math.sqrt(modes)
    rc, cc = row_coupling * scale, col_coupling
    pad = lambda m, lo: jnp.pad(m[:, :-1] if lo else m[:, 1:], ((0, 0), (1, 0) if lo else (0, 1)))
    kron = lambda a, b: (a[:, None, :, None] * b[None, :, None, :]).reshape(count, count)
    coupling = jnp.stack([kron(pad(rc, True), cc), kron(pad(rc, False), cc), kron(rc, pad(cc, True)), kron(rc, pad(cc, False))])
    own = (lax.axis_index("row") * nb + lax.axis_index("col")).reshape(1)

    payload, spectrum, hat, along = pl.pallas_call(
        functools.partial(first_kernel, width=width, modes=modes, count=count),
        out_shape=[
            jax.ShapeDtypeStruct((count, size), F32),
            jax.ShapeDtypeStruct((2, width, width), F32),
            jax.ShapeDtypeStruct((8 * modes, width), F32),
            jax.ShapeDtypeStruct((4 * modes, width), F32),
        ],
        in_specs=[SMEM] + [VMEM] * 6,
        out_specs=[VMEM] * 4,
        name="spectrum",
    )(wave_index, forcing, qh, ql, rows, lam_col, dirs)
    gathered = lax.all_to_all(payload, ("row", "col"), 0, 0, tiled=True)
    return pl.pallas_call(
        functools.partial(second_kernel, width=width, modes=modes, nb=nb),
        out_shape=jax.ShapeDtypeStruct((2, width, width), F32),
        in_specs=[SMEM, SMEM] + [VMEM] * 10 + [VMEM],
        out_specs=VMEM,
        name="sweeps",
    )(wave_index, own, gathered, spectrum, hat, along, coupling, mode_coupling, qh, ql, rows, lam_col, dirs_row)


def solution(mesh):
    return jax.shard_map(
        local,
        mesh=mesh,
        in_specs=(P(None, "row", "col"), P(), P(), P(), P(), P()),
        out_specs=P(None, "row", "col"),
        check_vma=False,
    )
```

profile of v0, /device:TPU:0, one launch (start us, length us, event | category | flops | bytes accessed | tf_op | source)
XLA Modules:
  0.0 35.9 jit_solution(8767519098842563300)
XLA Ops:
  0.0 0.0 copy-start.2
  0.7 0.0 copy-done.2
  0.7 0.7 %broadcast_in_dim.2.dirs = f32[32,128]{1,0:T(8,128)} broadcast(f32[32]{0:T(128)S(1)} %convert_element_type.11), dimensions={0} | broadcast | bytes 16512 | tf_op jit(solution)/shard_map/broadcast_in_dim | solution.py:349
  1.4 4.0 %spectrum.1 = (f32[32,2560]{1,0:T(8,128)}, f32[2,256,256]{2,1,0:T(8,128)}, f32[256,256]{1,0:T(8,128)}, f32[128,256]{1,0:T(8,128)}) custom-call(s32[1]{0:T(128)S(6)} %copy.15.wave, f32[2,256,256]{2,1,0:T(8,128)} %forcing.1, bf16[256,256]{1,0:T(8,128)(2,1)} %constant.23.clone.qh, bf16[256,256]{1,0:T(8,128)(2,1)} %constant.24.clone.ql, ...), custom_call_target="tpu_custom_call" | custom-call | tf_op jit(solution)/shard_map/spectrum/pallas_call | solution.py:359
  5.4 2.0 %copy.11 = f32[32,1,2560]{2,1,0:T(1,128)} copy(f32[32,1,2560]{2,0,1:T(8,128)} %bitcast.6) | data formatting | bytes 655360 | tf_op jit(solution)/shard_map/all_to_all | solution.py:371
  7.4 0.0 copy-start.1
  7.4 7.3 %all-to-all-start = ((f32[32,1,2560]{2,1,0:T(1,128)}), f32[32,1,2560]{2,1,0:T(1,128)S(1)}, u32[]{:S(2)}, u32[]{:S(2)}) async-start(f32[32,1,2560]{2,1,0:T(1,128)} %copy.11), calls=%async_computation | async-start | bytes 655360 | tf_op jit(solution)/shard_map/all_to_all | solution.py:371
  14.8 0.0 copy-done.1
  14.8 0.0 copy-start
  14.8 0.7 %copy-done = f32[8,8]{1,0:T(8,128)S(1)} copy-done((f32[8,8]{1,0:T(8,128)S(1)}, f32[8,8]{1,0:T(8,128)}, u32[]{:S(2)}) %copy-start) | copy-done | bytes 280
  15.5 0.1 fusion
  15.5 0.1 fusion.1
  15.6 0.7 %broadcast_in_dim_tile.3.dirs_row = f32[1,128]{1,0:T(1,128)} reshape(f32[4,32]{1,0:T(4,128)S(1)} %tile.2) | data formatting | bytes 1024 | tf_op jit(solution)/shard_map/broadcast_in_dim;tile | solution.py:350
  16.3 0.1 pad.16
  16.4 0.1 pad.18
  16.4 0.1 broadcast_multiply_fusion.1
  16.5 0.1 mul.106
  16.6 0.1 mul.109
  16.7 0.1 broadcast_multiply_fusion.3
  16.8 0.1 mul.99
  16.9 0.1 mul.102
  17.0 0.6 %pad_maximum_fusion.coupling = f32[4,32,32]{2,1,0:T(8,128)} fusion(f32[1,32,32]{2,1,0:T(8,128)S(1)} %mul.109, f32[1,32,32]{2,1,0:T(8,128)S(1)} %mul.106, f32[1,32,32]{2,1,0:T(8,128)S(1)} %mul.102, f32[1,32,32]{2,1,0:T(8,128)S(1)} %mul.99), kind=kLoop, calls=%fused_computation.1 | loop fusion | flops 12288 | bytes 32768 | tf_op jit(solution)/shard_map/stack | solution.py:356
  17.6 9.2 %all-to-all-done = f32[32,1,2560]{2,1,0:T(1,128)S(1)} async-done(((f32[32,1,2560]{2,1,0:T(1,128)}), f32[32,1,2560]{2,1,0:T(1,128)S(1)}, u32[]{:S(2)}, u32[]{:S(2)}) %all-to-all-start) | async-done | bytes 327712 | tf_op jit(solution)/shard_map/all_to_all | solution.py:371
  26.8 0.7 %copy.14 = f32[32,1,2560]{2,0,1:T(8,128)} copy(f32[32,1,2560]{2,1,0:T(1,128)S(1)} %all-to-all-done) | data formatting | bytes 655360
  27.5 8.3 %sweeps.1 = f32[2,256,256]{2,1,0:T(8,128)} custom-call(s32[1]{0:T(128)S(6)} %copy.15.wave, s32[1]{0:T(128)} %bitcast.own, f32[32,2560]{1,0:T(8,128)} %bitcast.5, f32[2,256,256]{2,1,0:T(8,128)} %get-tuple-element.10.spectrum, f32[256,256]{1,0:T(8,128)} %get-tuple-element.11.hat, f32[128,256]{1,0:T(8,128)} %get-tuple-element.12.along, ...), custom_call_target="tpu_custom_call" | custom-call | tf_op jit(solution)/shard_map/sweeps/pallas_call | solution.py:372
  (5 shorter events, 0.0 us)
Async XLA Ops:
  0.0 0.7 %copy-start.2 = (s32[32]{0:T(128)S(1)}, s32[32]{0:T(128)}, u32[]{:S(2)}) copy-start(s32[32]{0:T(128)} %param.12) | copy-start | bytes 388
  7.4 7.3 %copy-start.1 = (f32[4,4]{1,0:T(4,128)S(1)}, f32[4,4]{1,0:T(4,128)}, u32[]{:S(2)}) copy-start(f32[4,4]{1,0:T(4,128)} %param.13) | copy-start | bytes 196
  7.4 19.4 %all-to-all-start = ((f32[32,1,2560]{2,1,0:T(1,128)}), f32[32,1,2560]{2,1,0:T(1,128)S(1)}, u32[]{:S(2)}, u32[]{:S(2)}) async-start(f32[32,1,2560]{2,1,0:T(1,128)} %copy.11), calls=%async_computation | async-start | bytes 655360 | tf_op jit(solution)/shard_map/all_to_all | solution.py:371
  14.8 0.7 %copy-start = (f32[8,8]{1,0:T(8,128)S(1)}, f32[8,8]{1,0:T(8,128)}, u32[]{:S(2)}) copy-start(f32[8,8]{1,0:T(8,128)} %param.14) | copy-start | bytes 772
where the time goes:
time: 36.2 us; the launch traced here: 35.9 us
  Pallas kernels  12.4 us (34%)
  waiting for transfers between devices  9.16 us (25%)
  starting transfers between devices  7.33 us (20%)
  local copies, waits for them, and re-layouts  5.46 us (15%)
  other arithmetic  0.81 us (2%)
  between operations  0.74 us (2%)
    all_to_all x1, waiting for transfers between devices, local(): gathered = lax.all_to_all(payload, ('row', 'col'), 0, 0, tiled=True)  9.16 us
    pallas_call x1, Pallas kernels, local(): pl.pallas_call(functools.partial(second_kernel, width=width, modes=modes,...  8.35 us
    all_to_all x1, starting transfers between devices, local(): gathered = lax.all_to_all(payload, ('row', 'col'), 0, 0, tiled=True)  7.33 us
    pallas_call x1, Pallas kernels, local(): pl.pallas_call(functools.partial(first_kernel, width=width, modes=modes,...  4.04 us
    all_to_all x1, local copies, waits for them, and re-layouts, local(): gathered = lax.all_to_all(payload, ('row', 'col'), 0, 0, tiled=True)  2.04 us
    unnamed x7, local copies, waits for them, and re-layouts  1.43 us
  transfers between devices with their start and end apart: 1, of which 1 were waited for; matrix products, arithmetic and copies ran while one was open for 6% of the time, Pallas kernels for 0%

commit v1 on v0

--- a/solution.py
+++ b/solution.py
@@ -18,6 +18,7 @@
 NT = (((1,), (1,)), ((), ()))
 TN = (((0,), (0,)), ((), ()))
 VMEM = pl.BlockSpec(memory_space=pltpu.VMEM)
+HBM = pl.BlockSpec(memory_space=pltpu.HBM)
 SMEM = pl.BlockSpec(memory_space=pltpu.SMEM)
 
 
@@ -81,28 +82,64 @@
     return out[:count] + turn(out[count:], half)
 
 
-def first_kernel(wave, forcing, qh, ql, rows, lam_col, dirs, payload, spectrum, hat, along, *, width, modes, count):
-    kappa = KAPPA_UNIT * wave[0].astype(F32)
-    basis = (qh[...], ql[...])
+def turn_column(dirs, modes):
+    shape = (modes, modes)
+    spot = lax.broadcasted_iota(jnp.int32, shape, 0) == lanes(shape)
+    column = jnp.sum(jnp.where(spot, jnp.broadcast_to(dirs[...].astype(F32), shape), 0.0), 1, keepdims=True)
+    return 2.0 * math.pi / ANGLES * column
+
+
+def turn_row(dirs, modes):
+    shape = (modes, 4 * modes)
+    spot = (lax.broadcasted_iota(jnp.int32, shape, 0) == lanes(shape) % modes).astype(F32)
+    row = lax.dot_general(
+        jnp.broadcast_to(dirs[...].astype(F32), (8, modes)).astype(BF16), spot.astype(BF16), NN, preferred_element_type=F32
+    )
+    return 2.0 * math.pi / ANGLES * row[0:1]
+
+
+def first_kernel(
+    wave_in, dirs_in, forcing_in, qh_in, ql_in, rows_in, lam_in, payload_out, spectrum_out, hat_out, along_out,
+    wave, dirs, forcing, qh, ql, rows, lam_col, payload, spectrum, hat, along, arrived, left, *, width, modes, count
+):
+    sources = wave_in, dirs_in, qh_in, ql_in, forcing_in, rows_in, lam_in
+    targets = wave, dirs, qh, ql, forcing, rows, lam_col
+    copies = [pltpu.make_async_copy(a, b, arrived.at[k]) for k, (a, b) in enumerate(zip(sources, targets))]
+    for copy in copies:
+        copy.start()
+    for copy in copies[:2]:
+        copy.wait()
+    kappa = KAPPA_UNIT * wave[...].astype(F32)
     line = lanes((1, width)).astype(F32)
     ramp = (line + 0.5) / width
     windows = (1.0 - ramp, ramp)
-    theta = 2.0 * math.pi / ANGLES * dirs[...]
+    theta = turn_column(dirs, modes)
     tables = []
     for speed in (jnp.cos(theta), jnp.sin(theta)):
-        phase = kappa * speed[:, :1] * line
+        phase = kappa * speed * line
         cosine, sine = jnp.cos(phase), jnp.sin(phase)
         tables += [w * cosine for w in windows] + [-w * sine for w in windows]
     table = jnp.concatenate(tables, 0)
     along[...] = table[4 * modes :]
-    hats = dot(table, basis)
-    hat[...] = hats
-    across_hat, along_hat = split(hats[: 4 * modes]), split(hats[4 * modes :])
+    sends = [
+        pltpu.make_async_copy(a, b, left.at[k])
+        for k, (a, b) in enumerate(((along, along_out), (hat, hat_out), (spectrum, spectrum_out), (payload, payload_out)))
+    ]
+    sends[0].start()
+    for copy in copies[2:]:
+        copy.wait()
+    basis = (qh[...], ql[...])
+    hats = split(dot(table, basis))
+    hat[0], hat[1] = hats
+    sends[1].start()
+    across_hat = hats[0][: 4 * modes], hats[1][: 4 * modes]
+    along_hat = hats[0][4 * modes :], hats[1][4 * modes :]
 
     half_way = dot(forcing[...].reshape(2 * width, width), basis)
     coeff = [dot(basis, half_way[:width]), dot(basis, half_way[width:])]
     spectrum[0] = coeff[0]
     spectrum[1] = coeff[1]
+    sends[2].start()
     inv = inverse_symbol(lam_col[...], rows[4:5], kappa)
     coeff = [split(c) for c in cmul(coeff, inv)]
     weights = split(rows[...])
@@ -121,34 +158,36 @@
         proj = contract((rows_r, rows_i), table_hat)
         out += [proj[0:1], proj[1:2]]
     flat = jnp.concatenate(out + vectors, 1)
-    payload[...] = jnp.broadcast_to(flat, payload.shape)
-
-
-def second_kernel(
-    wave, own, gathered, spectrum, hat, along, coupling, mode, qh, ql, rows, lam_col, dirs_row, field, *, width, modes, nb
-):
-    count = gathered.shape[0]
-    kappa = KAPPA_UNIT * wave[0].astype(F32)
-    unknowns = 8 * modes
+    payload[...] = jnp.broadcast_to(flat[None], payload.shape)
+    sends[3].start()
+    for copy in sends:
+        copy.wait()
+
+
+def table_kernel(wave, mode, rows, lam_col, dirs, inv_out, diag_out, ends_out, mode_out, wave_out, *, width, modes):
+    kappa = KAPPA_UNIT * wave[...].astype(F32)
     half = 2 * modes
     inv = inverse_symbol(lam_col[...], rows[4:5], kappa)
     inv_split = split(inv[0]), split(inv[1])
+    for part in range(2):
+        for k in range(2):
+            inv_out[2 * part + k] = inv_split[part][k]
     sign = parity(width)
     q0, q1 = rows[0:1], rows[1:2]
-    robin_weight = q0, kappa * (q0 - q1)
     diag_rows = split(jnp.concatenate([q0 * q0, sign * q0 * q0, q0 * (q0 - q1), sign * q0 * (q0 - q1)] * 2, 0))
-    diag = dot(diag_rows, inv_split[0]), dot(diag_rows, inv_split[1])
-    same = diag[0][0:1], diag[1][0:1]
-    opposite = diag[0][1:2], diag[1][1:2]
-    same_robin = diag[0][0:1] - kappa * diag[1][2:3], diag[1][0:1] + kappa * diag[0][2:3]
-    opposite_robin = diag[0][1:2] - kappa * diag[1][3:4], diag[1][1:2] + kappa * diag[0][3:4]
-    hats = hat[...]
-    across_hat, along_hat = split(hats[: 2 * half]), split(hats[2 * half :])
-    tables = {"t": along_hat, "b": along_hat, "l": across_hat, "r": across_hat}
-    mode_split = split(mode[...])
+    real, imag = dot(diag_rows, inv_split[0]), dot(diag_rows, inv_split[1])
+    diag_out[...] = jnp.concatenate(
+        [
+            real[0:1], imag[0:1], real[1:2], imag[1:2],
+            real[0:1] - kappa * imag[2:3], imag[0:1] + kappa * real[2:3],
+            real[1:2] - kappa * imag[3:4], imag[1:2] + kappa * real[3:4],
+        ],
+        0,
+    )
+    mode_out[0], mode_out[1] = split(mode[...])
 
     lane = lanes((1, 4 * modes))
-    theta = 2.0 * math.pi / ANGLES * dirs_row[...]
+    theta = turn_row(dirs, modes)
     speeds = jnp.cos(theta), jnp.sin(theta)
     pick = lane // half, (lane // modes) % 2
 
@@ -158,11 +197,42 @@
         phase = kappa * speeds[axis] * float(x)
         return window * jnp.cos(phase), -window * jnp.sin(phase)
 
-    ends = {}
-    for side, axis, near, inner in (("t", 0, 0, 1), ("b", 0, width - 1, width - 2), ("l", 1, 0, 1), ("r", 1, width - 1, width - 2)):
+    ends = []
+    for axis, near, inner in ((0, 0, 1), (0, width - 1, width - 2), (1, 0, 1), (1, width - 1, width - 2)):
         e, n = wave_at(axis, near), wave_at(axis, inner)
         er, ei, nr, ni = e[0], -e[1], n[0], -n[1]
-        ends[side] = e, (er - kappa * (ei - ni), ei + kappa * (er - nr))
+        ends += [e[0], e[1], er - kappa * (ei - ni), ei + kappa * (er - nr)]
+    ends_out[...] = jnp.concatenate(ends, 0)
+    line = lax.broadcasted_iota(jnp.int32, (width, 1), 0).astype(F32)
+    ramp = (line + 0.5) / width
+    phase = kappa * speeds[0] * line
+    cosine, sine = jnp.cos(phase), jnp.sin(phase)
+    wave_out[0], wave_out[1] = (1.0 - ramp) * cosine, ramp * cosine
+    wave_out[2], wave_out[3] = (1.0 - ramp) * sine, ramp * sine
+
+
+def second_kernel(
+    wave, own, mine_in, other_in, spectrum, along, coupling, qh, ql, rows, lam_col, hats, invs, diags, end_rows, mode, waves, field,
+    *, width, modes, nb
+):
+    count = 2 * mine_in.shape[0]
+    kappa = KAPPA_UNIT * wave[...].astype(F32)
+    unknowns = 8 * modes
+    half = 2 * modes
+    lane = lanes((1, 4 * modes))
+    inv_split = (invs[0], invs[1]), (invs[2], invs[3])
+    sign = parity(width)
+    q0, q1 = rows[0:1], rows[1:2]
+    robin_weight = q0, kappa * (q0 - q1)
+    same, opposite, same_robin, opposite_robin = ((diags[2 * k : 2 * k + 1], diags[2 * k + 1 : 2 * k + 2]) for k in range(4))
+    across_hat = hats[0, : 2 * half], hats[1, : 2 * half]
+    along_hat = hats[0, 2 * half :], hats[1, 2 * half :]
+    tables = {"t": along_hat, "b": along_hat, "l": across_hat, "r": across_hat}
+    mode_split = mode[0], mode[1]
+    ends = {}
+    for k, side in enumerate("tblr"):
+        e = [end_rows[4 * k + j : 4 * k + j + 1] for j in range(4)]
+        ends[side] = (e[0], e[1]), (e[2], e[3])
     facing = {"t": "b", "b": "t", "l": "r", "r": "l"}
 
     def spread(proj, side):
@@ -251,7 +321,10 @@
             rob[b] = add(rob[b], cmul(g[b], same_robin), cmul(g[a], opposite_robin))
         return edge, rob
 
-    values = gathered[...]
+    mine_rows, other_rows = (r[...].reshape(count // 2, r.shape[2]) for r in (mine_in, other_in))
+    odd = own[0] // nb % 2 == 1
+    low_rows, high_rows = jnp.where(odd, other_rows, mine_rows), jnp.where(odd, mine_rows, other_rows)
+    values = jnp.concatenate([r[k : k + nb] for k in range(0, count // 2, nb) for r in (low_rows, high_rows)], 0)
     lanes_of = 4 * modes
     proj0 = {s: values[:, k * lanes_of : (k + 1) * lanes_of] for k, s in enumerate("tblr")}
     at = 4 * lanes_of
@@ -314,19 +387,14 @@
         left_rows = jnp.concatenate([q0, sq0, mine_g["l"][part], mine_g["r"][part], zero], 0)
         right_rows = jnp.concatenate([mine_g["t"][part], mine_g["b"][part], q0, sq0, zero], 0)
         coeff.append(spectrum[part] + dot(left_rows, right_rows, TN))
-    coeff = cmul(coeff, inv)
+    coeff = cmul(coeff, inverse_symbol(lam_col[...], rows[4:5], kappa))
     half_way = [dot(basis, coeff[0]), dot(basis, coeff[1])]
 
     cr, ci = c2[:, : 4 * modes], c2[:, 4 * modes :]
     low = lane < half
     flip = lambda a: pltpu.roll(a, half, 1)
     a0, a1 = jnp.where(low, cr, flip(ci)), jnp.where(low, flip(cr), ci)
-    line = lax.broadcasted_iota(jnp.int32, (width, 1), 0).astype(F32)
-    ramp = (line + 0.5) / width
-    phase = kappa * speeds[0] * line
-    plain = (1.0 - ramp) * a0 + ramp * a1
-    turned = (1.0 - ramp) * turn(a0, half) + ramp * turn(a1, half)
-    v = jnp.cos(phase) * plain + jnp.sin(phase) * turned
+    v = waves[0] * a0 + waves[1] * a1 + waves[2] * turn(a0, half) + waves[3] * turn(a1, half)
     along_split = split(along[...])
     field[0] = dot(half_way[0], basis) + dot(v, along_split)
     field[1] = dot(half_way[1], basis) + dot(-turn(v, half), along_split)
@@ -345,9 +413,7 @@
     rows = np.zeros((8, width), np.float32)
     rows[0], rows[1], rows[2], rows[3], rows[4] = basis[0], basis[1], sign * basis[0], sign * basis[1], values
     lam_col = np.ascontiguousarray(values[:, None])
-    turns = directions.astype(F32)
-    dirs = jnp.broadcast_to(turns[:, None], (modes, 128))
-    dirs_row = jnp.tile(turns, 4)[None, :]
+    wave, dirs = wave_index.reshape(1, 1), directions.reshape(1, modes)
 
     scale = 1.0 / math.sqrt(width) / math.sqrt(modes)
     rc, cc = row_coupling * scale, col_coupling
@@ -356,26 +422,63 @@
     coupling = jnp.stack([kron(pad(rc, True), cc), kron(pad(rc, False), cc), kron(rc, pad(cc, True)), kron(rc, pad(cc, False))])
     own = (lax.axis_index("row") * nb + lax.axis_index("col")).reshape(1)
 
+    fits = count <= 64
+    params = lambda mib: pltpu.CompilerParams(vmem_limit_bytes=mib << 20) if fits else None
     payload, spectrum, hat, along = pl.pallas_call(
         functools.partial(first_kernel, width=width, modes=modes, count=count),
         out_shape=[
-            jax.ShapeDtypeStruct((count, size), F32),
+            jax.ShapeDtypeStruct((count // 2, 1, size), F32),
             jax.ShapeDtypeStruct((2, width, width), F32),
-            jax.ShapeDtypeStruct((8 * modes, width), F32),
+            jax.ShapeDtypeStruct((2, 8 * modes, width), BF16),
             jax.ShapeDtypeStruct((4 * modes, width), F32),
         ],
-        in_specs=[SMEM] + [VMEM] * 6,
-        out_specs=[VMEM] * 4,
+        in_specs=[HBM] * 7,
+        out_specs=[HBM] * 4,
+        scratch_shapes=[
+            pltpu.VMEM((1, 1), jnp.int32),
+            pltpu.VMEM((1, modes), jnp.int32),
+            pltpu.VMEM((2, width, width), F32),
+            pltpu.VMEM((width, width), BF16),
+            pltpu.VMEM((width, width), BF16),
+            pltpu.VMEM((8, width), F32),
+            pltpu.VMEM((width, 1), F32),
+            pltpu.VMEM((count // 2, 1, size), F32),
+            pltpu.VMEM((2, width, width), F32),
+            pltpu.VMEM((2, 8 * modes, width), BF16),
+            pltpu.VMEM((4 * modes, width), F32),
+            pltpu.SemaphoreType.DMA((7,)),
+            pltpu.SemaphoreType.DMA((4,)),
+        ],
         name="spectrum",
-    )(wave_index, forcing, qh, ql, rows, lam_col, dirs)
-    gathered = lax.all_to_all(payload, ("row", "col"), 0, 0, tiled=True)
+    )(wave, dirs, forcing, qh, ql, rows, lam_col)
+    groups = [[a * nb + b for a in range(k, na, 2) for b in range(nb)] for k in range(2)]
+    mine = lax.all_to_all(payload, ("row", "col"), 0, 0, axis_index_groups=groups, tiled=True)
+    unknowns = mode_coupling.shape[0]
+    made = pl.pallas_call(
+        functools.partial(table_kernel, width=width, modes=modes),
+        out_shape=[
+            jax.ShapeDtypeStruct((4, width, width), BF16),
+            jax.ShapeDtypeStruct((8, width), F32),
+            jax.ShapeDtypeStruct((16, 4 * modes), F32),
+            jax.ShapeDtypeStruct((2, unknowns, unknowns), BF16),
+            jax.ShapeDtypeStruct((4, width, 4 * modes), F32),
+        ],
+        in_specs=[VMEM] * 5,
+        out_specs=[VMEM] * 5,
+        compiler_params=params(12),
+        cost_estimate=pl.CostEstimate(flops=1 << 30, bytes_accessed=1 << 21, transcendentals=1 << 18),
+        name="tables",
+    )(wave, mode_coupling, rows, lam_col, dirs)
+    mine, made, coupling = lax.optimization_barrier((mine, made, coupling))
+    other = lax.ppermute(mine, "row", [(a, a ^ 1) for a in range(na)])
     return pl.pallas_call(
         functools.partial(second_kernel, width=width, modes=modes, nb=nb),
         out_shape=jax.ShapeDtypeStruct((2, width, width), F32),
-        in_specs=[SMEM, SMEM] + [VMEM] * 10 + [VMEM],
+        in_specs=[VMEM, SMEM] + [VMEM] * 15,
         out_specs=VMEM,
+        compiler_params=params(28),
         name="sweeps",
-    )(wave_index, own, gathered, spectrum, hat, along, coupling, mode_coupling, qh, ql, rows, lam_col, dirs_row)
+    )(wave, own, mine, other, spectrum, along, coupling, qh, ql, rows, lam_col, hat, *made)
 
 
 def solution(mesh):

time: 36.2 us -> 29 us (0.80)
  local copies, waits for them, and re-layouts: 5.46 us -> 2.08 us
  waiting for transfers between devices: 9.16 us -> 5.86 us
  starting transfers between devices: 7.33 us -> 8.35 us
  Pallas kernels: 12.4 us -> 11.4 us
  other arithmetic: 0.81 us -> 0.19 us
    all_to_all x1, waiting for transfers between devices: 9.16 us -> 4.47 us  [local(): lax.all_to_all(payload, ('row', 'col'), 0, 0, axis_index_groups=groups, t...]
    all_to_all x1 -> x0, local copies, waits for them, and re-layouts: 2.04 us -> none  [local(): gathered = lax.all_to_all(payload, ('row', 'col'), 0, 0, tiled=True)]
    pallas_call x1, Pallas kernels: 8.35 us -> 6.38 us  [local(): pl.pallas_call(functools.partial(second_kernel, width=width, modes=modes,...]
    ppermute x0 -> x1, waiting for transfers between devices: none -> 1.39 us  [local(): other = lax.ppermute(mine, 'row', [(a, a ^ 1) for a in range(na)])]
    pallas_call x0 -> x1, Pallas kernels: none -> 1.12 us  [local(): pl.pallas_call(functools.partial(table_kernel, width=width, modes=modes),...]
    all_to_all x1, starting transfers between devices: 7.33 us -> 8.35 us  [local(): lax.all_to_all(payload, ('row', 'col'), 0, 0, axis_index_groups=groups, t...]
    broadcast_in_dim x1 -> x0, local copies, waits for them, and re-layouts: 0.67 us -> none  [local(): dirs = jnp.broadcast_to(turns[:, None], (modes, 128))]
    another operation x2 -> x0, local copies, waits for them, and re-layouts: 0.66 us -> none  [local(): dirs_row = jnp.tile(turns, 4)[None, :]]
  transfers between devices with their start and end apart: 1 -> 2, of which waited for: 1 -> 2; matrix products, arithmetic and copies ran while one was open for 6% -> 3% of each run, Pallas kernels for 0% -> 4%
where the time goes in v1:
time: 29 us; the launch traced here: 28.7 us
  Pallas kernels  11.4 us (39%)
  starting transfers between devices  8.35 us (29%)
  waiting for transfers between devices  5.86 us (20%)
  local copies, waits for them, and re-layouts  2.08 us (7%)
  between operations  0.79 us (3%)
    all_to_all x1, starting transfers between devices, local(): lax.all_to_all(payload, ('row', 'col'), 0, 0, axis_index_groups=groups, t...  8.35 us
    pallas_call x1, Pallas kernels, local(): pl.pallas_call(functools.partial(second_kernel, width=width, modes=modes,...  6.38 us
    all_to_all x1, waiting for transfers between devices, local(): lax.all_to_all(payload, ('row', 'col'), 0, 0, axis_index_groups=groups, t...  4.47 us
    pallas_call x1, Pallas kernels, local(): pl.pallas_call(functools.partial(first_kernel, width=width, modes=modes,...  3.92 us
    unnamed x22, local copies, waits for them, and re-layouts  1.41 us
    ppermute x1, waiting for transfers between devices, local(): other = lax.ppermute(mine, 'row', [(a, a ^ 1) for a in range(na)])  1.39 us
    pallas_call x1, Pallas kernels, local(): pl.pallas_call(functools.partial(table_kernel, width=width, modes=modes),...  1.12 us
  transfers between devices with their start and end apart: 2, of which 2 were waited for; matrix products, arithmetic and copies ran while one was open for 3% of the time, Pallas kernels for 4%

profile of v1, /device:TPU:0, one launch (start us, length us, event | category | flops | bytes accessed | tf_op | source)
XLA Modules:
  0.0 28.7 jit_solution(18249319201046289017)
XLA Ops:
  0.7 3.9 %spectrum.1 = (f32[16,1,2560]{2,1,0:T(1,128)}, f32[2,256,256]{2,1,0:T(8,128)}, bf16[2,256,256]{2,1,0:T(8,128)(2,1)}, f32[128,256]{1,0:T(8,128)}) custom-call(s32[1,1]{1,0:T(1,128)} %bitcast.3.wave_in, s32[1,32]{1,0:T(1,128)} %bitcast.6, f32[2,256,256]{2,1,0:T(8,128)} %forcing_in.1, bf16[256,256]{1,0:T(8,128)(2,1)} %constant.23.clone.qh_in.qh, ...), custom_call_target="tpu_custom_call" | custom-call | tf_op jit(solution)/shard_map/spectrum/pallas_call | solution.py:427
  4.6 0.0 copy-start.10
  4.6 8.4 %all-to-all-start = ((f32[16,1,2560]{2,1,0:T(1,128)}), f32[16,1,2560]{2,1,0:T(1,128)S(1)}, u32[]{:S(2)}, u32[]{:S(2)}) async-start(f32[16,1,2560]{2,1,0:T(1,128)} %get-tuple-element.21), calls=%async_computation | async-start | bytes 327680 | tf_op jit(solution)/shard_map/all_to_all | solution.py:455
  13.0 0.0 copy-done.10
  13.0 0.1 fusion.1
  13.0 0.1 pad.16
  13.1 0.7 %copy-done.9 = f32[8,8]{1,0:T(8,128)S(1)} copy-done((f32[8,8]{1,0:T(8,128)S(1)}, f32[8,8]{1,0:T(8,128)}, u32[]{:S(2)}) %copy-start.9) | copy-done | bytes 280
  13.8 0.1 fusion
  13.9 0.1 pad.18
  14.0 0.1 broadcast_multiply_fusion.1
  14.1 0.0 copy-start.8
  14.1 0.1 broadcast_multiply_fusion.3
  14.2 0.1 mul.106
  14.2 0.0 copy-start.1
  14.3 0.1 mul.109
  14.4 0.1 mul.99
  14.5 0.0 copy-start.6
  14.5 0.1 mul.102
  14.6 0.0 copy-start.7
  14.6 0.4 %copy-done.8 = f32[256,256]{1,0:T(8,128)S(1)} copy-done((f32[256,256]{1,0:T(8,128)S(1)}, f32[256,256]{1,0:T(8,128)}, u32[]{:S(2)}) %copy-start.8) | copy-done | bytes 262168
  15.0 0.2 copy-done.1
  15.2 0.0 copy-done.6
  15.2 0.1 copy-done.7
  15.3 1.1 %tables.1 = (bf16[4,256,256]{2,1,0:T(8,128)(2,1)S(1)}, f32[8,256]{1,0:T(8,128)S(1)}, f32[16,128]{1,0:T(8,128)S(1)}, bf16[2,256,256]{2,1,0:T(8,128)(2,1)S(1)}, f32[4,256,128]{2,1,0:T(8,128)S(1)}) custom-call(s32[1,1]{1,0:T(1,128)} %bitcast.4.wave, f32[256,256]{1,0:T(8,128)S(1)} %copy-done.8, f32[8,256]{1,0:T(8,128)S(1)} %copy-done.6, f32[256,1]{1,0:T(8,128)S(1)} %copy-done.1, ...), custom_call_target="tpu_custom_call" | custom-call | flops 1073741824 | bytes 2097152 | tf_op jit(solution)/shard_map/tables/pallas_call | solution.py:457
  16.4 0.0 copy-start.2
  16.4 4.5 %all-to-all-done.mine_in = f32[16,1,2560]{2,1,0:T(1,128)S(1)} async-done(((f32[16,1,2560]{2,1,0:T(1,128)}), f32[16,1,2560]{2,1,0:T(1,128)S(1)}, u32[]{:S(2)}, u32[]{:S(2)}) %all-to-all-start) | async-done | bytes 163872 | tf_op jit(solution)/shard_map/all_to_all | solution.py:455
  20.9 0.0 collective-permute-start
  20.9 1.4 %collective-permute-done.other_in = f32[16,1,2560]{2,1,0:T(1,128)S(1)} collective-permute-done((f32[16,1,2560]{2,1,0:T(1,128)S(1)}, f32[16,1,2560]{2,1,0:T(1,128)S(1)}, u32[]{:S(2)}, u32[]{:S(2)}) %collective-permute-start) | collective-permute-done | bytes 163872 | tf_op jit(solution)/shard_map/ppermute | solution.py:473
  22.3 0.0 copy-done
  22.3 0.0 copy-done.5
  22.3 0.0 copy-done.2
  22.3 6.4 %sweeps.1 = f32[2,256,256]{2,1,0:T(8,128)} custom-call(s32[1,1]{1,0:T(1,128)} %bitcast.5.wave, s32[1]{0:T(128)} %bitcast.1.own, f32[16,1,2560]{2,1,0:T(1,128)S(1)} %all-to-all-done.mine_in, f32[16,1,2560]{2,1,0:T(1,128)S(1)} %collective-permute-done.other_in, f32[2,256,256]{2,1,0:T(8,128)S(1)} %copy-done, f32[128,256]{1,0:T(8,128)S(1)} %copy-done.5, ...), custom_call_target="tpu_custom_call" | custom-call | tf_op jit(solution)/shard_map/sweeps/pallas_call | solution.py:474
  (11 shorter events, 0.0 us)
Async XLA Ops:
  4.6 8.4 %copy-start.10 = (f32[4,4]{1,0:T(4,128)S(1)}, f32[4,4]{1,0:T(4,128)}, u32[]{:S(2)}) copy-start(f32[4,4]{1,0:T(4,128)} %param.13) | copy-start | bytes 196
  4.6 16.3 %all-to-all-start = ((f32[16,1,2560]{2,1,0:T(1,128)}), f32[16,1,2560]{2,1,0:T(1,128)S(1)}, u32[]{:S(2)}, u32[]{:S(2)}) async-start(f32[16,1,2560]{2,1,0:T(1,128)} %get-tuple-element.21), calls=%async_computation | async-start | bytes 327680 | tf_op jit(solution)/shard_map/all_to_all | solution.py:455
  13.1 0.7 %copy-start.9 = (f32[8,8]{1,0:T(8,128)S(1)}, f32[8,8]{1,0:T(8,128)}, u32[]{:S(2)}) copy-start(f32[8,8]{1,0:T(8,128)} %param.14) | copy-start | bytes 772
  14.1 1.0 %copy-start.8 = (f32[256,256]{1,0:T(8,128)S(1)}, f32[256,256]{1,0:T(8,128)}, u32[]{:S(2)}) copy-start(f32[256,256]{1,0:T(8,128)} %mode.1) | copy-start | bytes 786436
  14.2 0.9 %copy-start.1 = (f32[256,1]{1,0:T(8,128)S(1)}, f32[256,1]{1,0:T(8,128)}, u32[]{:S(2)}) copy-start(f32[256,1]{1,0:T(8,128)} %constant.26.clone.lam_in.lam_col) | copy-start | bytes 3076
  14.5 0.7 %copy-start.6 = (f32[8,256]{1,0:T(8,128)S(1)}, f32[8,256]{1,0:T(8,128)}, u32[]{:S(2)}) copy-start(f32[8,256]{1,0:T(8,128)} %constant.25.clone.rows_in.rows) | copy-start | bytes 24580
  14.6 0.7 %copy-start.7 = (s32[32]{0:T(128)S(1)}, s32[32]{0:T(128)}, u32[]{:S(2)}) copy-start(s32[32]{0:T(128)} %param.12) | copy-start | bytes 388
  15.3 7.0 %copy-start = (f32[2,256,256]{2,1,0:T(8,128)S(1)}, f32[2,256,256]{2,1,0:T(8,128)}, u32[]{:S(2)}) copy-start(f32[2,256,256]{2,1,0:T(8,128)} %get-tuple-element.28.spectrum) | copy-start | bytes 1572868
  15.3 7.0 %copy-start.3 = (bf16[256,256]{1,0:T(8,128)(2,1)S(1)}, bf16[256,256]{1,0:T(8,128)(2,1)}, u32[]{:S(2)}) copy-start(bf16[256,256]{1,0:T(8,128)(2,1)} %constant.23.clone.qh_in.qh) | copy-start | bytes 393220
  15.3 7.0 %copy-start.4 = (bf16[2,256,256]{2,1,0:T(8,128)(2,1)S(1)}, bf16[2,256,256]{2,1,0:T(8,128)(2,1)}, u32[]{:S(2)}) copy-start(bf16[2,256,256]{2,1,0:T(8,128)(2,1)} %get-tuple-element.31.hats) | copy-start | bytes 786436
  15.3 7.0 %copy-start.5 = (f32[128,256]{1,0:T(8,128)S(1)}, f32[128,256]{1,0:T(8,128)}, u32[]{:S(2)}) copy-start(f32[128,256]{1,0:T(8,128)} %get-tuple-element.29.along) | copy-start | bytes 393220
  16.4 5.9 %copy-start.2 = (bf16[256,256]{1,0:T(8,128)(2,1)S(1)}, bf16[256,256]{1,0:T(8,128)(2,1)}, u32[]{:S(2)}) copy-start(bf16[256,256]{1,0:T(8,128)(2,1)} %constant.24.clone.ql_in.ql) | copy-start | bytes 393220
  20.9 1.4 %collective-permute-start = (f32[16,1,2560]{2,1,0:T(1,128)S(1)}, f32[16,1,2560]{2,1,0:T(1,128)S(1)}, u32[]{:S(2)}, u32[]{:S(2)}) collective-permute-start(f32[16,1,2560]{2,1,0:T(1,128)S(1)} %all-to-all-done.mine_in), channel_id=1, source_target_pairs={{0,8},{8,0},{16,24},{24,16},{1,9},{9,1},{17,25},{25,17},{2,10},{10... | collective-permute-start | bytes 491528 | tf_op jit(solution)/shard_map/ppermute | solution.py:473

commit v2 on v1

--- a/solution.py
+++ b/solution.py
@@ -33,6 +33,13 @@
     ah, al = split(a)
     bh, bl = split(b)
     mul = functools.partial(lax.dot_general, dimension_numbers=dims, preferred_element_type=F32)
+    (da,), (db,) = dims[0]
+    size = ah.shape[1 - da]
+    if size <= 256 and da == 1 and size % 8 == 0:
+        both = mul(jnp.concatenate([ah.astype(F32), al.astype(F32)], 0).astype(BF16), bh)
+        return both[:size] + (both[size:] + mul(ah, bl))
+    if ah.shape[da] % 128 == 0:
+        return mul(jnp.concatenate([ah, al, ah], da), jnp.concatenate([bh, bh, bl], db))
     return mul(ah, bh) + (mul(ah, bl) + mul(al, bh))
 
 
@@ -164,7 +171,9 @@
         copy.wait()
 
 
-def table_kernel(wave, mode, rows, lam_col, dirs, inv_out, diag_out, ends_out, mode_out, wave_out, *, width, modes):
+def table_kernel(
+    wave, mode, rows, lam_col, dirs, spectrum, qh, ql, inv_out, diag_out, ends_out, mode_out, wave_out, still, *, width, modes
+):
     kappa = KAPPA_UNIT * wave[...].astype(F32)
     half = 2 * modes
     inv = inverse_symbol(lam_col[...], rows[4:5], kappa)
@@ -186,6 +195,11 @@
     )
     mode_out[0], mode_out[1] = split(mode[...])
 
+    basis = (qh[...], ql[...])
+    coeff = cmul((spectrum[0], spectrum[1]), inv)
+    for part in range(2):
+        still[part] = dot(dot(basis, coeff[part]), basis)
+
     lane = lanes((1, 4 * modes))
     theta = turn_row(dirs, modes)
     speeds = jnp.cos(theta), jnp.sin(theta)
@@ -204,16 +218,44 @@
         ends += [e[0], e[1], er - kappa * (ei - ni), ei + kappa * (er - nr)]
     ends_out[...] = jnp.concatenate(ends, 0)
     line = lax.broadcasted_iota(jnp.int32, (width, 1), 0).astype(F32)
-    ramp = (line + 0.5) / width
     phase = kappa * speeds[0] * line
-    cosine, sine = jnp.cos(phase), jnp.sin(phase)
-    wave_out[0], wave_out[1] = (1.0 - ramp) * cosine, ramp * cosine
-    wave_out[2], wave_out[3] = (1.0 - ramp) * sine, ramp * sine
+    wave_out[0], wave_out[1] = jnp.cos(phase), jnp.sin(phase)
+
+
+def side_kernel(rows, hats, invs, diag, along, qh, ql, jump_out, green_out, along_out, *, width, modes):
+    half = 2 * modes
+    inv_split = (invs[0], invs[1]), (invs[2], invs[3])
+    sign = parity(width)
+    q0 = rows[0:1]
+    basis = (qh[...].astype(F32) + ql[...].astype(F32)) * q0
+    pair = split(jnp.concatenate([basis, basis * sign], 0))
+    for part in range(2):
+        made = dot(pair, inv_split[part])
+        green_out[part], green_out[2 + part] = made[:width], made[width:]
+    along_out[0], along_out[1] = split(along[...])
+    table = hats[0].astype(F32) + hats[1].astype(F32)
+    weighted = table * q0
+    stacked = split(jnp.concatenate([weighted, weighted * sign], 0))
+    br, bi = dot(stacked, inv_split[0]), dot(stacked, inv_split[1])
+    for part, (a, b) in enumerate((("l", "tblr"), ("t", "lrtb"))):
+        start = 4 * modes * part
+        real, imag = slice(start, start + half), slice(start + half, start + 2 * half)
+        blocks = {}
+        for k, src in enumerate(b[:2]):
+            off = 8 * modes * k
+            r, i = slice(real.start + off, real.stop + off), slice(imag.start + off, imag.stop + off)
+            blocks[src] = (br[r] - bi[i]) * q0, (br[i] + bi[r]) * q0
+        for k, src in enumerate(b[2:]):
+            blocks[src] = cmul((table[real], table[imag]), (diag[2 * k : 2 * k + 1], diag[2 * k + 1 : 2 * k + 2]))
+        for k, src in enumerate("tblr"):
+            high, low = split(jnp.concatenate(blocks[src], 0))
+            jump_out[0, start : start + 2 * half, k * width : (k + 1) * width] = high
+            jump_out[1, start : start + 2 * half, k * width : (k + 1) * width] = low
 
 
 def second_kernel(
-    wave, own, mine_in, other_in, spectrum, along, coupling, qh, ql, rows, lam_col, hats, invs, diags, end_rows, mode, waves, field,
-    *, width, modes, nb
+    wave, own, mine_in, other_in, coupling, picks, rows, hats, invs, diags, end_rows, mode, waves, still,
+    jump_table, green, along, qh, ql, field, *, width, modes, nb
 ):
     count = 2 * mine_in.shape[0]
     kappa = KAPPA_UNIT * wave[...].astype(F32)
@@ -270,10 +312,10 @@
         out = dot(stacked, table)
         return [(out[2 * k * size : (2 * k + 1) * size], out[(2 * k + 1) * size : (2 * k + 2) * size]) for k in range(len(zs))]
 
-    def coarse_of(projs):
+    def coarse_of(weights, projs):
         total = 0.0
         for k, side in enumerate("tblr"):
-            total = total + dot(coupling[k], spread(projs[side], side))
+            total = total + spread(dot(weights[k], projs[side]), side)
         return dot(total, mode_split, NT)
 
     def robin_of(c, base):
@@ -304,22 +346,30 @@
     def scale(r, z):
         return r * z[0], r * z[1]
 
-    def responses(g):
-        edge, rob = {}, {}
-        for (a, b), (c, d) in ((("t", "b"), ("l", "r")), (("l", "r"), ("t", "b"))):
-            vectors = []
-            for src in (a, b):
-                plain, heavy = scale(q0, g[src]), cmul(g[src], robin_weight)
-                vectors += [plain, scale(sign, plain), heavy, scale(sign, heavy)]
-            x = apply_inverse(vectors)
-            cross = [scale(q0, add(x[k], scale(sign, x[k + 4]))) for k in range(4)]
-            edge[c], edge[d], rob[c], rob[d] = cross
+    jump_split = jump_table[0], jump_table[1]
+
+    def project_sources(rows_of):
+        flip = lambda z: scale(sign, z)
+        kinds = [
+            [rows_of("lt", src) for src in "tblr"],
+            [flip(rows_of("r", "t")), flip(rows_of("r", "b")), rows_of("r", "r"), rows_of("r", "l")],
+            [rows_of("b", "b"), rows_of("b", "t"), flip(rows_of("b", "l")), flip(rows_of("b", "r"))],
+        ]
+        size = kinds[0][0][0].shape[0]
+        stacked = jnp.concatenate([jnp.concatenate([z[part] for z in kind], 1) for part in range(2) for kind in kinds], 0)
+        x = dot(stacked, jump_split, NT)
+        block = lambda k, at: (
+            x[k * size : (k + 1) * size, at : at + 2 * half] + turn(x[(k + 3) * size : (k + 4) * size, at : at + 2 * half], half)
+        )
+        return {"l": block(0, 0), "t": block(0, 2 * half), "r": block(1, 0), "b": block(2, 2 * half)}
+
+    def project_sent(sent):
+        out = {}
         for a, b in (("t", "b"), ("l", "r")):
-            edge[a] = add(edge[a], cmul(g[a], same), cmul(g[b], opposite))
-            edge[b] = add(edge[b], cmul(g[b], same), cmul(g[a], opposite))
-            rob[a] = add(rob[a], cmul(g[a], same_robin), cmul(g[b], opposite_robin))
-            rob[b] = add(rob[b], cmul(g[b], same_robin), cmul(g[a], opposite_robin))
-        return edge, rob
+            size = sent[a][0].shape[0]
+            both = contract([jnp.concatenate([sent[a][k], sent[b][k]], 0) for k in range(2)], tables[a])
+            out[a], out[b] = both[:size], both[size:]
+        return out
 
     mine_rows, other_rows = (r[...].reshape(count // 2, r.shape[2]) for r in (mine_in, other_in))
     odd = own[0] // nb % 2 == 1
@@ -333,71 +383,59 @@
         robin0[s] = values[:, at : at + width], values[:, at + width : at + 2 * width]
         at += 2 * width
 
-    out1 = robin_of(coarse_of(proj0), robin0)
-    edge, rob = responses(incoming(out1))
-    proj1 = {}
-    for a, b in (("t", "b"), ("l", "r")):
-        ja, jb = sub(edge[a], out1[a]), sub(edge[b], out1[b])
-        both = contract((jnp.concatenate([ja[0], jb[0]], 0), jnp.concatenate([ja[1], jb[1]], 0)), tables[a])
-        proj1[a], proj1[b] = proj0[a] + both[:count], proj0[b] + both[count:]
-    base = {s: add(robin0[s], rob[s]) for s in "tblr"}
-    out2 = robin_of(coarse_of(proj1), base)
-    g2 = incoming(out2)
-
-    mine = own[0]
-    picks = [coupling[k, pl.ds(mine, 1), :] for k in range(4)]
-    one = (lanes((1, count)) == mine).astype(F32)
-    weights = split(jnp.concatenate(picks + [one] * 4, 0))
-    mixed = {s: (dot(weights, g2[s][0]), dot(weights, g2[s][1])) for s in "tblr"}
-    sent = {s: (dot(weights, out2[s][0]), dot(weights, out2[s][1])) for s in "tblr"}
-    base0 = {s: dot(weights, proj0[s]) for s in "tblr"}
+    couplings = [split(coupling[k]) for k in range(4)]
+    out1 = robin_of(coarse_of(couplings, proj0), robin0)
+    g1 = incoming(out1)
+    share, sent = project_sources(lambda o, src: g1[src]), project_sent(out1)
+    proj1 = {s: proj0[s] + share[s] - sent[s] for s in "tblr"}
+    pick = [split(picks[k]) for k in range(4)]
+    base = {s: (dot(pick[k], robin0[s][0]), dot(pick[k], robin0[s][1])) for k, s in enumerate("tblr")}
+    base_proj = {s: dot(pick[k], proj0[s]) for k, s in enumerate("tblr")}
+    every = jnp.concatenate([picks[k] for k in range(4)], 0)
+    every_split = split(every)
+    mixed1 = {s: (dot(every_split, g1[s][0]), dot(every_split, g1[s][1])) for s in "tblr"}
+    group = lambda z, k: (z[0][8 * k : 8 * k + 8], z[1][8 * k : 8 * k + 8])
+    vectors = []
+    for k, s in enumerate("tblr"):
+        for src in "lr" if s in "tb" else "tb":
+            z = cmul(group(mixed1[src], k), robin_weight)
+            vectors.append(scale(sign, z) if s in "br" else z)
+    x = apply_inverse(vectors)
+    for k, s in enumerate("tblr"):
+        cross = scale(q0, add(x[2 * k], scale(sign, x[2 * k + 1])))
+        near, far = group(mixed1[s], k), group(mixed1[facing[s]], k)
+        base[s] = add(base[s], cross, cmul(near, same_robin), cmul(far, opposite_robin))
+    c1 = coarse_of([split(dot(every_split, couplings[k])) for k in range(4)], proj1)
+    tb = synth([outgoing(c1[8 * k : 8 * k + 8], s) for k, s in ((0, "t"), (1, "b"))], along_hat)
+    lr = synth([outgoing(c1[8 * k : 8 * k + 8], s) for k, s in ((2, "l"), (3, "r"))], across_hat)
+    out2 = {s: add(base[s], z) for s, z in zip("tblr", tb + lr)}
+
     index = {"t": 0, "b": 1, "l": 2, "r": 3}
     rowof = lambda z, k: (z[0][k : k + 1], z[1][k : k + 1])
-    vectors = []
-    order = []
+
+    share, sent = project_sources(lambda o, src: out2[facing[src]]), project_sent(out2)
+    total = jnp.zeros((1, unknowns), F32)
     for o in "tblr":
-        weight = scale(sign, (q0, q0)) if o in "br" else (q0, q0)
-        for src in ("lr" if o in "tb" else "tb"):
-            z = rowof(mixed[src], index[o])
-            vectors.append((weight[0] * z[0], weight[0] * z[1]))
-            order.append((o, src))
-    x = apply_inverse(vectors)
-    total = jnp.zeros((1, unknowns), F32)
-    jumps = {}
-    for o in "tblr":
-        k = 2 * index[o]
-        e = scale(q0, add(x[k], scale(sign, x[k + 1])))
-        e = add(e, cmul(rowof(mixed[o], index[o]), same), cmul(rowof(mixed[facing[o]], index[o]), opposite))
-        jumps[o] = sub(e, rowof(sent[o], index[o]))
-    for a, b in (("t", "b"), ("l", "r")):
-        rr = jnp.concatenate([jumps[a][0], jumps[b][0]] + [jumps[a][0]] * 6, 0)
-        ri = jnp.concatenate([jumps[a][1], jumps[b][1]] + [jumps[a][1]] * 6, 0)
-        both = contract((rr, ri), tables[a])
-        for j, o in enumerate((a, b)):
-            k = index[o]
-            total = total + spread(base0[o][k : k + 1] + both[j : j + 1], o)
+        total = total + spread(base_proj[o][5:6] + share[o][index[o] : index[o] + 1] - sent[o][5:6], o)
     c2 = dot(jnp.broadcast_to(total, (8, unknowns)), mode_split, NT)[0:1]
 
-    mine_g = {s: rowof(mixed[s], 4) for s in "tblr"}
+    mine_g = {s: rowof(out2[facing[s]], 4) for s in "tblr"}
     basis = (qh[...], ql[...])
-    coeff = []
-    zero = jnp.zeros((4, width), F32)
-    sq0 = sign * q0
-    for part in range(2):
-        left_rows = jnp.concatenate([q0, sq0, mine_g["l"][part], mine_g["r"][part], zero], 0)
-        right_rows = jnp.concatenate([mine_g["t"][part], mine_g["b"][part], q0, sq0, zero], 0)
-        coeff.append(spectrum[part] + dot(left_rows, right_rows, TN))
-    coeff = cmul(coeff, inverse_symbol(lam_col[...], rows[4:5], kappa))
-    half_way = [dot(basis, coeff[0]), dot(basis, coeff[1])]
+    near, far = (green[0], green[1]), (green[2], green[3])
+    across_rows = add(cmul(near, mine_g["t"]), cmul(far, mine_g["b"]))
+    across_cols = add(cmul(near, mine_g["l"]), cmul(far, mine_g["r"]))
+    solved = [still[k] + dot(across_rows[k], basis) + dot(basis, across_cols[k], NT) for k in range(2)]
 
     cr, ci = c2[:, : 4 * modes], c2[:, 4 * modes :]
     low = lane < half
     flip = lambda a: pltpu.roll(a, half, 1)
     a0, a1 = jnp.where(low, cr, flip(ci)), jnp.where(low, flip(cr), ci)
-    v = waves[0] * a0 + waves[1] * a1 + waves[2] * turn(a0, half) + waves[3] * turn(a1, half)
-    along_split = split(along[...])
-    field[0] = dot(half_way[0], basis) + dot(v, along_split)
-    field[1] = dot(half_way[1], basis) + dot(-turn(v, half), along_split)
+    ramp = (lax.broadcasted_iota(jnp.int32, (width, 1), 0).astype(F32) + 0.5) / width
+    blend = lambda lo, hi: lo + ramp * (hi - lo)
+    v = waves[0] * blend(a0, a1) + waves[1] * blend(turn(a0, half), turn(a1, half))
+    along_split = along[0], along[1]
+    field[0] = solved[0] + dot(v, along_split)
+    field[1] = solved[1] + dot(-turn(v, half), along_split)
 
 
 def local(forcing, wave_index, directions, row_coupling, col_coupling, mode_coupling):
@@ -421,6 +459,20 @@
     kron = lambda a, b: (a[:, None, :, None] * b[None, :, None, :]).reshape(count, count)
     coupling = jnp.stack([kron(pad(rc, True), cc), kron(pad(rc, False), cc), kron(rc, pad(cc, True)), kron(rc, pad(cc, False))])
     own = (lax.axis_index("row") * nb + lax.axis_index("col")).reshape(1)
+    tile = jnp.arange(count)
+    taken = lax.dynamic_slice_in_dim(coupling, own[0], 1, 1)[:, 0]
+    sums = jnp.concatenate([taken, (tile == own[0]).astype(F32)[None]])
+    ahead = lambda m, by: jnp.pad(m[:, by:], ((0, 0), (0, by)))
+    behind = lambda m, by: jnp.pad(m[:, :-by], ((0, 0), (by, 0)))
+    moved = jnp.stack(
+        [
+            behind(sums, nb),
+            ahead(sums, nb),
+            jnp.where(tile % nb == 0, 0.0, behind(sums, 1)),
+            jnp.where(tile % nb == nb - 1, 0.0, ahead(sums, 1)),
+        ]
+    )
+    picks = jnp.concatenate([moved, taken[:, None], jnp.zeros((4, 2, count), F32)], 1)
 
     fits = count <= 64
     params = lambda mib: pltpu.CompilerParams(vmem_limit_bytes=mib << 20) if fits else None
@@ -454,31 +506,48 @@
     groups = [[a * nb + b for a in range(k, na, 2) for b in range(nb)] for k in range(2)]
     mine = lax.all_to_all(payload, ("row", "col"), 0, 0, axis_index_groups=groups, tiled=True)
     unknowns = mode_coupling.shape[0]
-    made = pl.pallas_call(
+    estimate = pl.CostEstimate(flops=1 << 30, bytes_accessed=1 << 21, transcendentals=1 << 18)
+    invs, diags, ends, mode, waves, still = pl.pallas_call(
         functools.partial(table_kernel, width=width, modes=modes),
         out_shape=[
             jax.ShapeDtypeStruct((4, width, width), BF16),
             jax.ShapeDtypeStruct((8, width), F32),
             jax.ShapeDtypeStruct((16, 4 * modes), F32),
             jax.ShapeDtypeStruct((2, unknowns, unknowns), BF16),
-            jax.ShapeDtypeStruct((4, width, 4 * modes), F32),
+            jax.ShapeDtypeStruct((2, width, 4 * modes), F32),
+            jax.ShapeDtypeStruct((2, width, width), F32),
         ],
-        in_specs=[VMEM] * 5,
-        out_specs=[VMEM] * 5,
-        compiler_params=params(12),
-        cost_estimate=pl.CostEstimate(flops=1 << 30, bytes_accessed=1 << 21, transcendentals=1 << 18),
+        in_specs=[VMEM] * 8,
+        out_specs=[VMEM] * 6,
+        compiler_params=params(16),
+        cost_estimate=estimate,
         name="tables",
-    )(wave, mode_coupling, rows, lam_col, dirs)
-    mine, made, coupling = lax.optimization_barrier((mine, made, coupling))
+    )(wave, mode_coupling, rows, lam_col, dirs, spectrum, qh, ql)
+    mine, invs, diags, ends, mode, waves, still, coupling, picks, hat, along = lax.optimization_barrier(
+        (mine, invs, diags, ends, mode, waves, still, coupling, picks, hat, along)
+    )
     other = lax.ppermute(mine, "row", [(a, a ^ 1) for a in range(na)])
+    jumps, green, along = pl.pallas_call(
+        functools.partial(side_kernel, width=width, modes=modes),
+        out_shape=[
+            jax.ShapeDtypeStruct((2, 8 * modes, 4 * width), BF16),
+            jax.ShapeDtypeStruct((4, width, width), F32),
+            jax.ShapeDtypeStruct((2, 4 * modes, width), BF16),
+        ],
+        in_specs=[VMEM] * 7,
+        out_specs=[VMEM] * 3,
+        compiler_params=params(16),
+        cost_estimate=estimate,
+        name="sides",
+    )(rows, hat, invs, diags, along, qh, ql)
     return pl.pallas_call(
         functools.partial(second_kernel, width=width, modes=modes, nb=nb),
         out_shape=jax.ShapeDtypeStruct((2, width, width), F32),
-        in_specs=[VMEM, SMEM] + [VMEM] * 15,
+        in_specs=[VMEM, SMEM] + [VMEM] * 17,
         out_specs=VMEM,
         compiler_params=params(28),
         name="sweeps",
-    )(wave, own, mine, other, spectrum, along, coupling, qh, ql, rows, lam_col, hat, *made)
+    )(wave, own, mine, other, coupling, picks, rows, hat, invs, diags, ends, mode, waves, still, jumps, green, along, qh, ql)
 
 
 def solution(mesh):

time: 29 us -> 27.6 us (0.952)
  waiting for transfers between devices: 5.86 us -> 4.39 us
  local copies, waits for them, and re-layouts: 2.08 us -> 1.73 us
    pallas_call x1, Pallas kernels: 6.38 us -> 4.99 us  [local(): pl.pallas_call(functools.partial(second_kernel, width=width, modes=modes,...]
    ppermute x1, waiting for transfers between devices: 1.39 us -> 0.24 us  [local(): other = lax.ppermute(mine, 'row', [(a, a ^ 1) for a in range(na)])]
    pallas_call x0 -> x1, Pallas kernels: none -> 1.14 us  [local(): pl.pallas_call(functools.partial(side_kernel, width=width, modes=modes),...]
    unnamed x22 -> x25, local copies, waits for them, and re-layouts: 1.41 us -> 0.73 us
    pallas_call x1, Pallas kernels: 1.12 us -> 1.55 us  [local(): pl.pallas_call(functools.partial(table_kernel, width=width, modes=modes),...]
    all_to_all x1, waiting for transfers between devices: 4.47 us -> 4.16 us  [local(): lax.all_to_all(payload, ('row', 'col'), 0, 0, axis_index_groups=groups, t...]
  transfers between devices with their start and end apart: 2 -> 2, of which waited for: 2 -> 2; matrix products, arithmetic and copies ran while one was open for 3% -> 5% of each run, Pallas kernels for 4% -> 10%
where the time goes in v2:
time: 27.6 us; the launch traced here: 27.3 us
  Pallas kernels  11.4 us (41%)
  starting transfers between devices  8.49 us (31%)
  waiting for transfers between devices  4.39 us (16%)
  local copies, waits for them, and re-layouts  1.73 us (6%)
  between operations  0.87 us (3%)
  other arithmetic  0.35 us (1%)
    all_to_all x1, starting transfers between devices, local(): lax.all_to_all(payload, ('row', 'col'), 0, 0, axis_index_groups=groups, t...  8.48 us
    pallas_call x1, Pallas kernels, local(): pl.pallas_call(functools.partial(second_kernel, width=width, modes=modes,...  4.99 us
    all_to_all x1, waiting for transfers between devices, local(): lax.all_to_all(payload, ('row', 'col'), 0, 0, axis_index_groups=groups, t...  4.16 us
    pallas_call x1, Pallas kernels, local(): pl.pallas_call(functools.partial(first_kernel, width=width, modes=modes,...  3.77 us
    pallas_call x1, Pallas kernels, local(): pl.pallas_call(functools.partial(table_kernel, width=width, modes=modes),...  1.55 us
    pallas_call x1, Pallas kernels, local(): pl.pallas_call(functools.partial(side_kernel, width=width, modes=modes),...  1.14 us
    unnamed x25, local copies, waits for them, and re-layouts  0.73 us
  transfers between devices with their start and end apart: 2, of which 2 were waited for; matrix products, arithmetic and copies ran while one was open for 5% of the time, Pallas kernels for 10%

profile of v2, /device:TPU:0, one launch (start us, length us, event | category | flops | bytes accessed | tf_op | source)
XLA Modules:
  0.0 27.3 jit_solution(8587056755253931681)
XLA Ops:
  0.7 3.8 %spectrum.1 = (f32[16,1,2560]{2,1,0:T(1,128)}, f32[2,256,256]{2,1,0:T(8,128)}, bf16[2,256,256]{2,1,0:T(8,128)(2,1)}, f32[128,256]{1,0:T(8,128)}) custom-call(s32[1,1]{1,0:T(1,128)} %bitcast.12.wave_in, s32[1,32]{1,0:T(1,128)} %bitcast.15, f32[2,256,256]{2,1,0:T(8,128)} %forcing_in.1, bf16[256,256]{1,0:T(8,128)(2,1)} %constant.46.clone.qh_in.qh, ...), custom_call_target="tpu_custom_call" | custom-call | tf_op jit(solution)/shard_map/spectrum/pallas_call | solution.py:479
  4.4 0.0 copy-start.10
  4.4 0.0 copy-start.9
  4.5 0.0 copy-start.7
  4.5 8.5 %all-to-all-start = ((f32[16,1,2560]{2,1,0:T(1,128)}), f32[16,1,2560]{2,1,0:T(1,128)S(1)}, u32[]{:S(2)}, u32[]{:S(2)}) async-start(f32[16,1,2560]{2,1,0:T(1,128)} %get-tuple-element.29), calls=%async_computation | async-start | bytes 327680 | tf_op jit(solution)/shard_map/all_to_all | solution.py:507
  13.0 0.1 fusion.3
  13.1 0.1 pad.32
  13.2 0.1 fusion.2
  13.3 0.1 pad.34
  13.3 0.1 broadcast_multiply_fusion
  13.4 0.1 mul.109
  13.5 0.1 mul.106
  13.6 0.0 copy-start.4
  13.6 0.1 broadcast_multiply_fusion.2
  13.7 0.0 copy-start.3
  13.8 0.1 mul.102
  13.9 0.1 mul.99
  14.0 0.1 fusion.1
  14.1 0.1 fusion
  14.2 0.1 pad.45.clone
  14.3 0.1 pad_bitcast_fusion
  14.3 0.1 select_bitcast_fusion
  14.4 0.3 copy-done.3
  14.7 0.1 copy-done.1
  14.8 0.1 copy-done
  14.9 0.2 copy-done.5
  15.1 1.5 %tables.1 = (bf16[4,256,256]{2,1,0:T(8,128)(2,1)S(1)}, f32[8,256]{1,0:T(8,128)S(1)}, f32[16,128]{1,0:T(8,128)S(1)}, bf16[2,256,256]{2,1,0:T(8,128)(2,1)S(1)}, f3...) custom-call(s32[1,1]{1,0:T(1,128)} %bitcast.13.wave, f32[256,256]{1,0:T(8,128)S(1)} %copy-done.7, ...), custom_call_target="tpu_custom_call" | custom-call | flops 1073741824 | bytes 2097152 | tf_op jit(solution)/shard_map/tables/pallas_call | solution.py:510
  16.7 0.1 maximum_maximum_fusion.picks
  16.7 4.2 %all-to-all-done.mine_in = f32[16,1,2560]{2,1,0:T(1,128)S(1)} async-done(((f32[16,1,2560]{2,1,0:T(1,128)}), f32[16,1,2560]{2,1,0:T(1,128)S(1)}, u32[]{:S(2)}, u32[]{:S(2)}) %all-to-all-start) | async-done | bytes 163872 | tf_op jit(solution)/shard_map/all_to_all | solution.py:507
  20.9 1.1 %sides.1 = (bf16[2,256,1024]{2,1,0:T(8,128)(2,1)S(1)}, f32[4,256,256]{2,1,0:T(8,128)S(1)}, bf16[2,128,256]{2,1,0:T(8,128)(2,1)S(1)}) custom-call(f32[8,256]{1,0:T(8,128)S(1)} %copy-done.4, bf16[2,256,256]{2,1,0:T(8,128)(2,1)S(1)} %copy-done.2, bf16[4,256,256]{2,1,0:T(8,128)(2,1)S(1)} %get-tuple-element.43.invs, f32[8,256]{1,0:T(8,128)S(1)} %get-tuple-element.44.diag.diags, ...), custom_call_target="tpu_custom_call" | custom-call | flops 1073741824 | bytes 2097152 | tf_op jit(solution)/shard_map/sides/pallas_call | solution.py:530
  22.0 0.2 collective-permute-done.other_in
  22.3 5.0 %sweeps.1 = f32[2,256,256]{2,1,0:T(8,128)} custom-call(s32[1,1]{1,0:T(1,128)} %bitcast.14.wave, s32[1]{0:T(128)} %bitcast.1.own, f32[16,1,2560]{2,1,0:T(1,128)S(1)} %all-to-all-done.mine_in, f32[16,1,2560]{2,1,0:T(1,128)S(1)} %collective-permute-done.other_in, f32[4,32,32]{2,1,0:T(8,128)S(1)} %constant_dynamic-update-slice_fusion.coupling, ...), custom_call_target="tpu_custom_call" | custom-call | tf_op jit(solution)/shard_map/sweeps/pallas_call | solution.py:543
  (27 shorter events, 0.1 us)
Async XLA Ops:
  4.4 8.6 %copy-start.10 = (f32[4,4]{1,0:T(4,128)S(1)}, f32[4,4]{1,0:T(4,128)}, u32[]{:S(2)}) copy-start(f32[4,4]{1,0:T(4,128)} %param.13) | copy-start | bytes 196
  4.4 8.8 %copy-start.9 = (f32[8,8]{1,0:T(8,128)S(1)}, f32[8,8]{1,0:T(8,128)}, u32[]{:S(2)}) copy-start(f32[8,8]{1,0:T(8,128)} %param.14) | copy-start | bytes 772
  4.5 10.0 %copy-start.7 = (f32[256,256]{1,0:T(8,128)S(1)}, f32[256,256]{1,0:T(8,128)}, u32[]{:S(2)}) copy-start(f32[256,256]{1,0:T(8,128)} %mode.1) | copy-start | bytes 786436
  4.5 16.4 %all-to-all-start = ((f32[16,1,2560]{2,1,0:T(1,128)}), f32[16,1,2560]{2,1,0:T(1,128)S(1)}, u32[]{:S(2)}, u32[]{:S(2)}) async-start(f32[16,1,2560]{2,1,0:T(1,128)} %get-tuple-element.29), calls=%async_computation | async-start | bytes 327680 | tf_op jit(solution)/shard_map/all_to_all | solution.py:507
  13.0 1.5 %copy-start.6 = (f32[2,256,256]{2,1,0:T(8,128)S(1)}, f32[2,256,256]{2,1,0:T(8,128)}, u32[]{:S(2)}) copy-start(f32[2,256,256]{2,1,0:T(8,128)} %get-tuple-element.30.spectrum) | copy-start | bytes 1572868
  13.6 0.8 %copy-start.4 = (f32[8,256]{1,0:T(8,128)S(1)}, f32[8,256]{1,0:T(8,128)}, u32[]{:S(2)}) copy-start(f32[8,256]{1,0:T(8,128)} %constant.48.clone.rows_in.rows) | copy-start | bytes 24580
  13.7 0.9 %copy-start.3 = (f32[256,1]{1,0:T(8,128)S(1)}, f32[256,1]{1,0:T(8,128)}, u32[]{:S(2)}) copy-start(f32[256,1]{1,0:T(8,128)} %constant.49.clone.lam_in.lam_col) | copy-start | bytes 3076
  13.8 1.0 %copy-start.1 = (bf16[256,256]{1,0:T(8,128)(2,1)S(1)}, bf16[256,256]{1,0:T(8,128)(2,1)}, u32[]{:S(2)}) copy-start(bf16[256,256]{1,0:T(8,128)(2,1)} %constant.46.clone.qh_in.qh) | copy-start | bytes 393220
  14.0 0.9 %copy-start = (bf16[256,256]{1,0:T(8,128)(2,1)S(1)}, bf16[256,256]{1,0:T(8,128)(2,1)}, u32[]{:S(2)}) copy-start(bf16[256,256]{1,0:T(8,128)(2,1)} %constant.47.clone.ql_in.ql) | copy-start | bytes 393220
  14.4 0.7 %copy-start.5 = (s32[32]{0:T(128)S(1)}, s32[32]{0:T(128)}, u32[]{:S(2)}) copy-start(s32[32]{0:T(128)} %param.12) | copy-start | bytes 388
  15.1 5.8 %copy-start.2 = (bf16[2,256,256]{2,1,0:T(8,128)(2,1)S(1)}, bf16[2,256,256]{2,1,0:T(8,128)(2,1)}, u32[]{:S(2)}) copy-start(bf16[2,256,256]{2,1,0:T(8,128)(2,1)} %get-tuple-element.42.hats) | copy-start | bytes 786436
  15.1 5.8 %copy-start.8 = (f32[128,256]{1,0:T(8,128)S(1)}, f32[128,256]{1,0:T(8,128)}, u32[]{:S(2)}) copy-start(f32[128,256]{1,0:T(8,128)} %get-tuple-element.49.along) | copy-start | bytes 393220
  20.9 1.4 %collective-permute-start = (f32[16,1,2560]{2,1,0:T(1,128)S(1)}, f32[16,1,2560]{2,1,0:T(1,128)S(1)}, u32[]{:S(2)}, u32[]{:S(2)}) collective-permute-start(f32[16,1,2560]{2,1,0:T(1,128)S(1)} %all-to-all-done.mine_in), channel_id=1, source_target_pairs={{0,8},{8,0},{16,24},{24,16},{1,9},{9,1},{17,25},{25,17},{2,10},{10... | collective-permute-start | bytes 491528 | tf_op jit(solution)/shard_map/ppermute | solution.py:529

commit v3 on v2

--- a/solution.py
+++ b/solution.py
@@ -83,9 +83,9 @@
     return sign * pltpu.roll(z, half, 1)
 
 
-def contract(rows, table):
-    count, half = rows[0].shape[0], table[0].shape[0] // 2
-    out = dot(jnp.concatenate(rows, 0), table, NT)
+def contract(rows, table, dims=NT):
+    count, half = rows[0].shape[0], table[0].shape[1 - dims[0][1][0]] // 2
+    out = dot(jnp.concatenate(rows, 0), table, dims)
     return out[:count] + turn(out[count:], half)
 
 
@@ -105,9 +105,21 @@
     return 2.0 * math.pi / ANGLES * row[0:1]
 
 
+def wave_table(kappa, theta, width):
+    line = lanes((1, width)).astype(F32)
+    ramp = (line + 0.5) / width
+    windows = (1.0 - ramp, ramp)
+    tables = []
+    for speed in (jnp.cos(theta), jnp.sin(theta)):
+        phase = kappa * speed * line
+        cosine, sine = jnp.cos(phase), jnp.sin(phase)
+        tables += [w * cosine for w in windows] + [-w * sine for w in windows]
+    return jnp.concatenate(tables, 0)
+
+
 def first_kernel(
-    wave_in, dirs_in, forcing_in, qh_in, ql_in, rows_in, lam_in, payload_out, spectrum_out, hat_out, along_out,
-    wave, dirs, forcing, qh, ql, rows, lam_col, payload, spectrum, hat, along, arrived, left, *, width, modes, count
+    wave_in, dirs_in, forcing_in, qh_in, ql_in, rows_in, lam_in, payload,
+    wave, dirs, forcing, qh, ql, rows, lam_col, arrived, *, width, modes
 ):
     sources = wave_in, dirs_in, qh_in, ql_in, forcing_in, rows_in, lam_in
     targets = wave, dirs, qh, ql, forcing, rows, lam_col
@@ -117,36 +129,16 @@
     for copy in copies[:2]:
         copy.wait()
     kappa = KAPPA_UNIT * wave[...].astype(F32)
-    line = lanes((1, width)).astype(F32)
-    ramp = (line + 0.5) / width
-    windows = (1.0 - ramp, ramp)
-    theta = turn_column(dirs, modes)
-    tables = []
-    for speed in (jnp.cos(theta), jnp.sin(theta)):
-        phase = kappa * speed * line
-        cosine, sine = jnp.cos(phase), jnp.sin(phase)
-        tables += [w * cosine for w in windows] + [-w * sine for w in windows]
-    table = jnp.concatenate(tables, 0)
-    along[...] = table[4 * modes :]
-    sends = [
-        pltpu.make_async_copy(a, b, left.at[k])
-        for k, (a, b) in enumerate(((along, along_out), (hat, hat_out), (spectrum, spectrum_out), (payload, payload_out)))
-    ]
-    sends[0].start()
+    table = wave_table(kappa, turn_column(dirs, modes), width)
     for copy in copies[2:]:
         copy.wait()
     basis = (qh[...], ql[...])
     hats = split(dot(table, basis))
-    hat[0], hat[1] = hats
-    sends[1].start()
     across_hat = hats[0][: 4 * modes], hats[1][: 4 * modes]
     along_hat = hats[0][4 * modes :], hats[1][4 * modes :]
 
     half_way = dot(forcing[...].reshape(2 * width, width), basis)
     coeff = [dot(basis, half_way[:width]), dot(basis, half_way[width:])]
-    spectrum[0] = coeff[0]
-    spectrum[1] = coeff[1]
-    sends[2].start()
     inv = inverse_symbol(lam_col[...], rows[4:5], kappa)
     coeff = [split(c) for c in cmul(coeff, inv)]
     weights = split(rows[...])
@@ -166,13 +158,11 @@
         out += [proj[0:1], proj[1:2]]
     flat = jnp.concatenate(out + vectors, 1)
     payload[...] = jnp.broadcast_to(flat[None], payload.shape)
-    sends[3].start()
-    for copy in sends:
-        copy.wait()
 
 
 def table_kernel(
-    wave, mode, rows, lam_col, dirs, spectrum, qh, ql, inv_out, diag_out, ends_out, mode_out, wave_out, still, *, width, modes
+    wave, mode, rows, lam_col, dirs, forcing, qh, ql,
+    inv_out, diag_out, ends_out, mode_out, wave_out, still, hat_out, along_out, *, width, modes
 ):
     kappa = KAPPA_UNIT * wave[...].astype(F32)
     half = 2 * modes
@@ -196,9 +186,13 @@
     mode_out[0], mode_out[1] = split(mode[...])
 
     basis = (qh[...], ql[...])
-    coeff = cmul((spectrum[0], spectrum[1]), inv)
+    half_way = dot(forcing[...].reshape(2 * width, width), basis)
+    coeff = cmul((dot(basis, half_way[:width]), dot(basis, half_way[width:])), inv)
     for part in range(2):
         still[part] = dot(dot(basis, coeff[part]), basis)
+    table = wave_table(kappa, turn_column(dirs, modes), width)
+    along_out[0], along_out[1] = split(table[4 * modes :])
+    hat_out[0], hat_out[1] = split(dot(table, basis))
 
     lane = lanes((1, 4 * modes))
     theta = turn_row(dirs, modes)
@@ -222,7 +216,7 @@
     wave_out[0], wave_out[1] = jnp.cos(phase), jnp.sin(phase)
 
 
-def side_kernel(rows, hats, invs, diag, along, qh, ql, jump_out, green_out, along_out, *, width, modes):
+def side_kernel(rows, cols, hats, invs, diag_rows, qh, ql, jump_out, green_out, turned_out, *, width, modes):
     half = 2 * modes
     inv_split = (invs[0], invs[1]), (invs[2], invs[3])
     sign = parity(width)
@@ -232,30 +226,31 @@
     for part in range(2):
         made = dot(pair, inv_split[part])
         green_out[part], green_out[2 + part] = made[:width], made[width:]
-    along_out[0], along_out[1] = split(along[...])
     table = hats[0].astype(F32) + hats[1].astype(F32)
+    turned = table.T
+    turned_out[0], turned_out[1] = split(turned)
     weighted = table * q0
     stacked = split(jnp.concatenate([weighted, weighted * sign], 0))
-    br, bi = dot(stacked, inv_split[0]), dot(stacked, inv_split[1])
-    for part, (a, b) in enumerate((("l", "tblr"), ("t", "lrtb"))):
-        start = 4 * modes * part
-        real, imag = slice(start, start + half), slice(start + half, start + 2 * half)
+    real, imag = dot(inv_split[0], stacked, NT), dot(inv_split[1], stacked, NT)
+    diag = diag_rows[...].T
+    size = 2 * half
+    for part, sources in enumerate(("tblr", "lrtb")):
+        at = slice(size * part, size * part + size)
         blocks = {}
-        for k, src in enumerate(b[:2]):
-            off = 8 * modes * k
-            r, i = slice(real.start + off, real.stop + off), slice(imag.start + off, imag.stop + off)
-            blocks[src] = (br[r] - bi[i]) * q0, (br[i] + bi[r]) * q0
-        for k, src in enumerate(b[2:]):
-            blocks[src] = cmul((table[real], table[imag]), (diag[2 * k : 2 * k + 1], diag[2 * k + 1 : 2 * k + 2]))
+        for k, src in enumerate(sources[:2]):
+            off = slice(at.start + 2 * size * k, at.stop + 2 * size * k)
+            blocks[src] = (real[:, off] + turn(imag[:, off], half)) * cols[...]
+        for k, src in enumerate(sources[2:]):
+            blocks[src] = turned[:, at] * diag[:, 2 * k : 2 * k + 1] + turn(turned[:, at], half) * diag[:, 2 * k + 1 : 2 * k + 2]
         for k, src in enumerate("tblr"):
-            high, low = split(jnp.concatenate(blocks[src], 0))
-            jump_out[0, start : start + 2 * half, k * width : (k + 1) * width] = high
-            jump_out[1, start : start + 2 * half, k * width : (k + 1) * width] = low
+            high, low = split(blocks[src])
+            jump_out[0, k * width : (k + 1) * width, at] = high
+            jump_out[1, k * width : (k + 1) * width, at] = low
 
 
 def second_kernel(
     wave, own, mine_in, other_in, coupling, picks, rows, hats, invs, diags, end_rows, mode, waves, still,
-    jump_table, green, along, qh, ql, field, *, width, modes, nb
+    jump_table, green, turned, along, qh, ql, field, *, width, modes, nb
 ):
     count = 2 * mine_in.shape[0]
     kappa = KAPPA_UNIT * wave[...].astype(F32)
@@ -269,7 +264,9 @@
     same, opposite, same_robin, opposite_robin = ((diags[2 * k : 2 * k + 1], diags[2 * k + 1 : 2 * k + 2]) for k in range(4))
     across_hat = hats[0, : 2 * half], hats[1, : 2 * half]
     along_hat = hats[0, 2 * half :], hats[1, 2 * half :]
-    tables = {"t": along_hat, "b": along_hat, "l": across_hat, "r": across_hat}
+    across_turned = turned[0, :, : 2 * half], turned[1, :, : 2 * half]
+    along_turned = turned[0, :, 2 * half :], turned[1, :, 2 * half :]
+    tables = {"t": along_turned, "l": across_turned}
     mode_split = mode[0], mode[1]
     ends = {}
     for k, side in enumerate("tblr"):
@@ -357,7 +354,7 @@
         ]
         size = kinds[0][0][0].shape[0]
         stacked = jnp.concatenate([jnp.concatenate([z[part] for z in kind], 1) for part in range(2) for kind in kinds], 0)
-        x = dot(stacked, jump_split, NT)
+        x = dot(stacked, jump_split)
         block = lambda k, at: (
             x[k * size : (k + 1) * size, at : at + 2 * half] + turn(x[(k + 3) * size : (k + 4) * size, at : at + 2 * half], half)
         )
@@ -367,7 +364,7 @@
         out = {}
         for a, b in (("t", "b"), ("l", "r")):
             size = sent[a][0].shape[0]
-            both = contract([jnp.concatenate([sent[a][k], sent[b][k]], 0) for k in range(2)], tables[a])
+            both = contract([jnp.concatenate([sent[a][k], sent[b][k]], 0) for k in range(2)], tables[a], NN)
             out[a], out[b] = both[:size], both[size:]
         return out
 
@@ -450,7 +447,7 @@
     sign = 1.0 - 2.0 * (np.arange(width) % 2)
     rows = np.zeros((8, width), np.float32)
     rows[0], rows[1], rows[2], rows[3], rows[4] = basis[0], basis[1], sign * basis[0], sign * basis[1], values
-    lam_col = np.ascontiguousarray(values[:, None])
+    lam_col, col = values[:, None], basis[0][:, None]
     wave, dirs = wave_index.reshape(1, 1), directions.reshape(1, modes)
 
     scale = 1.0 / math.sqrt(width) / math.sqrt(modes)
@@ -476,16 +473,11 @@
 
     fits = count <= 64
     params = lambda mib: pltpu.CompilerParams(vmem_limit_bytes=mib << 20) if fits else None
-    payload, spectrum, hat, along = pl.pallas_call(
-        functools.partial(first_kernel, width=width, modes=modes, count=count),
-        out_shape=[
-            jax.ShapeDtypeStruct((count // 2, 1, size), F32),
-            jax.ShapeDtypeStruct((2, width, width), F32),
-            jax.ShapeDtypeStruct((2, 8 * modes, width), BF16),
-            jax.ShapeDtypeStruct((4 * modes, width), F32),
-        ],
+    payload = pl.pallas_call(
+        functools.partial(first_kernel, width=width, modes=modes),
+        out_shape=jax.ShapeDtypeStruct((count // 2, 1, size), F32),
         in_specs=[HBM] * 7,
-        out_specs=[HBM] * 4,
+        out_specs=VMEM,
         scratch_shapes=[
             pltpu.VMEM((1, 1), jnp.int32),
             pltpu.VMEM((1, modes), jnp.int32),
@@ -494,12 +486,7 @@
             pltpu.VMEM((width, width), BF16),
             pltpu.VMEM((8, width), F32),
             pltpu.VMEM((width, 1), F32),
-            pltpu.VMEM((count // 2, 1, size), F32),
-            pltpu.VMEM((2, width, width), F32),
-            pltpu.VMEM((2, 8 * modes, width), BF16),
-            pltpu.VMEM((4 * modes, width), F32),
             pltpu.SemaphoreType.DMA((7,)),
-            pltpu.SemaphoreType.DMA((4,)),
         ],
         name="spectrum",
     )(wave, dirs, forcing, qh, ql, rows, lam_col)
@@ -507,7 +494,7 @@
     mine = lax.all_to_all(payload, ("row", "col"), 0, 0, axis_index_groups=groups, tiled=True)
     unknowns = mode_coupling.shape[0]
     estimate = pl.CostEstimate(flops=1 << 30, bytes_accessed=1 << 21, transcendentals=1 << 18)
-    invs, diags, ends, mode, waves, still = pl.pallas_call(
+    invs, diags, ends, mode, waves, still, hat, along = pl.pallas_call(
         functools.partial(table_kernel, width=width, modes=modes),
         out_shape=[
             jax.ShapeDtypeStruct((4, width, width), BF16),
@@ -516,38 +503,40 @@
             jax.ShapeDtypeStruct((2, unknowns, unknowns), BF16),
             jax.ShapeDtypeStruct((2, width, 4 * modes), F32),
             jax.ShapeDtypeStruct((2, width, width), F32),
+            jax.ShapeDtypeStruct((2, 8 * modes, width), BF16),
+            jax.ShapeDtypeStruct((2, 4 * modes, width), BF16),
         ],
         in_specs=[VMEM] * 8,
-        out_specs=[VMEM] * 6,
+        out_specs=[VMEM] * 8,
         compiler_params=params(16),
         cost_estimate=estimate,
         name="tables",
-    )(wave, mode_coupling, rows, lam_col, dirs, spectrum, qh, ql)
+    )(wave, mode_coupling, rows, lam_col, dirs, forcing, qh, ql)
     mine, invs, diags, ends, mode, waves, still, coupling, picks, hat, along = lax.optimization_barrier(
         (mine, invs, diags, ends, mode, waves, still, coupling, picks, hat, along)
     )
     other = lax.ppermute(mine, "row", [(a, a ^ 1) for a in range(na)])
-    jumps, green, along = pl.pallas_call(
+    jumps, green, turned = pl.pallas_call(
         functools.partial(side_kernel, width=width, modes=modes),
         out_shape=[
-            jax.ShapeDtypeStruct((2, 8 * modes, 4 * width), BF16),
+            jax.ShapeDtypeStruct((2, 4 * width, 8 * modes), BF16),
             jax.ShapeDtypeStruct((4, width, width), F32),
-            jax.ShapeDtypeStruct((2, 4 * modes, width), BF16),
+            jax.ShapeDtypeStruct((2, width, 8 * modes), BF16),
         ],
         in_specs=[VMEM] * 7,
         out_specs=[VMEM] * 3,
         compiler_params=params(16),
         cost_estimate=estimate,
         name="sides",
-    )(rows, hat, invs, diags, along, qh, ql)
+    )(rows, col, hat, invs, diags, qh, ql)
     return pl.pallas_call(
         functools.partial(second_kernel, width=width, modes=modes, nb=nb),
         out_shape=jax.ShapeDtypeStruct((2, width, width), F32),
-        in_specs=[VMEM, SMEM] + [VMEM] * 17,
+        in_specs=[VMEM, SMEM] + [VMEM] * 18,
         out_specs=VMEM,
         compiler_params=params(28),
         name="sweeps",
-    )(wave, own, mine, other, coupling, picks, rows, hat, invs, diags, ends, mode, waves, still, jumps, green, along, qh, ql)
+    )(wave, own, mine, other, coupling, picks, rows, hat, invs, diags, ends, mode, waves, still, jumps, green, turned, along, qh, ql)
 
 
 def solution(mesh):

time: 27.6 us -> 27.2 us (0.986)
  waiting for transfers between devices: 4.39 us -> 3.01 us
  Pallas kernels: 11.4 us -> 12.5 us
    pallas_call x1, Pallas kernels: 1.55 us -> 2.9 us  [local(): pl.pallas_call(functools.partial(table_kernel, width=width, modes=modes),...]
    all_to_all x1, waiting for transfers between devices: 4.16 us -> 2.82 us  [local(): lax.all_to_all(payload, ('row', 'col'), 0, 0, axis_index_groups=groups, t...]
    pallas_call x1, Pallas kernels: 4.99 us -> 4.63 us  [local(): pl.pallas_call(functools.partial(second_kernel, width=width, modes=modes,...]
    unnamed x25 -> x23, local copies, waits for them, and re-layouts: 0.73 us -> 0.73 us
  transfers between devices with their start and end apart: 2 -> 2, of which waited for: 2 -> 2; matrix products, arithmetic and copies ran while one was open for 5% -> 5% of each run, Pallas kernels for 10% -> 15%
where the time goes in v3:
time: 27.2 us; the launch traced here: 26.9 us
  Pallas kernels  12.5 us (46%)
  starting transfers between devices  8.49 us (31%)
  waiting for transfers between devices  3.01 us (11%)
  local copies, waits for them, and re-layouts  1.72 us (6%)
  between operations  0.86 us (3%)
  other arithmetic  0.35 us (1%)
    all_to_all x1, starting transfers between devices, local(): lax.all_to_all(payload, ('row', 'col'), 0, 0, axis_index_groups=groups, t...  8.48 us
    pallas_call x1, Pallas kernels, local(): pl.pallas_call(functools.partial(second_kernel, width=width, modes=modes,...  4.63 us
    pallas_call x1, Pallas kernels, local(): pl.pallas_call(functools.partial(first_kernel, width=width, modes=modes),...  3.74 us
    pallas_call x1, Pallas kernels, local(): pl.pallas_call(functools.partial(table_kernel, width=width, modes=modes),...  2.9 us
    all_to_all x1, waiting for transfers between devices, local(): lax.all_to_all(payload, ('row', 'col'), 0, 0, axis_index_groups=groups, t...  2.82 us
    pallas_call x1, Pallas kernels, local(): pl.pallas_call(functools.partial(side_kernel, width=width, modes=modes),...  1.19 us
    unnamed x23, local copies, waits for them, and re-layouts  0.73 us
  transfers between devices with their start and end apart: 2, of which 2 were waited for; matrix products, arithmetic and copies ran while one was open for 5% of the time, Pallas kernels for 15%

profile of v3, /device:TPU:0, one launch (start us, length us, event | category | flops | bytes accessed | tf_op | source)
XLA Modules:
  0.0 26.9 jit_solution(2048454520468685211)
XLA Ops:
  0.7 3.7 %spectrum.1 = f32[16,1,2560]{2,1,0:T(1,128)} custom-call(s32[1,1]{1,0:T(1,128)} %bitcast.12.wave_in, s32[1,32]{1,0:T(1,128)} %bitcast.15, f32[2,256,256]{2,1,0:T(8,128)} %forcing.1, bf16[256,256]{1,0:T(8,128)(2,1)} %constant.48.clone.qh_in.qh, bf16[256,256]{1,0:T(8,128)(2,1)} %constant.49.clone.ql_in.ql, f32[8,256]{1,0:T(8,128)} %constant.50.clone.rows_in.rows, ...), custom_call_target="tpu_custom_call" | custom-call | tf_op jit(solution)/shard_map/spectrum/pallas_call | solution.py:476
  4.4 0.0 copy-start.9
  4.4 0.0 copy-start.8
  4.4 0.0 copy-start.6
  4.4 8.5 %all-to-all-start = ((f32[16,1,2560]{2,1,0:T(1,128)}), f32[16,1,2560]{2,1,0:T(1,128)S(1)}, u32[]{:S(2)}, u32[]{:S(2)}) async-start(f32[16,1,2560]{2,1,0:T(1,128)} %spectrum.1), calls=%async_computation | async-start | bytes 327680 | tf_op jit(solution)/shard_map/all_to_all | solution.py:494
  13.0 0.1 fusion.3
  13.1 0.1 pad.32
  13.2 0.1 fusion.2
  13.3 0.1 pad.34
  13.3 0.1 broadcast_multiply_fusion
  13.4 0.1 mul.109
  13.5 0.1 mul.106
  13.6 0.0 copy-start.3
  13.6 0.1 broadcast_multiply_fusion.2
  13.7 0.1 mul.102
  13.8 0.1 mul.99
  14.0 0.1 fusion.1
  14.1 0.1 fusion
  14.2 0.1 pad.45.clone
  14.2 0.1 pad_bitcast_fusion
  14.3 0.1 select_bitcast_fusion
  14.4 0.2 copy-done.3
  14.6 0.2 copy-done.1
  14.8 0.1 copy-done
  14.9 0.2 copy-done.4
  15.0 0.0 copy-done.5
  15.1 2.9 %tables.1 = (bf16[4,256,256]{2,1,0:T(8,128)(2,1)S(1)}, f32[8,256]{1,0:T(8,128)S(1)}, f32[16,128]{1,0:T(8,128)S(1)}, bf16[2,256,256]{2,1,0:T(8,128)(2,1)S(1)}, f3...) custom-call(s32[1,1]{1,0:T(1,128)} %bitcast.13.wave, ...), custom_call_target="tpu_custom_call" | custom-call | flops 1073741824 | bytes 2097152 | tf_op jit(solution)/shard_map/tables/pallas_call | solution.py:497
  18.0 0.1 maximum_maximum_fusion.picks
  18.1 2.8 %all-to-all-done.mine_in = f32[16,1,2560]{2,1,0:T(1,128)S(1)} async-done(((f32[16,1,2560]{2,1,0:T(1,128)}), f32[16,1,2560]{2,1,0:T(1,128)S(1)}, u32[]{:S(2)}, u32[]{:S(2)}) %all-to-all-start) | async-done | bytes 163872 | tf_op jit(solution)/shard_map/all_to_all | solution.py:494
  20.9 1.2 %sides.1 = (bf16[2,1024,256]{2,1,0:T(8,128)(2,1)S(1)}, f32[4,256,256]{2,1,0:T(8,128)S(1)}, bf16[2,256,256]{2,1,0:T(8,128)(2,1)S(1)}) custom-call(f32[8,256]{1,0:T(8,128)S(1)} %copy-done.4, f32[256,1]{1,0:T(8,128)S(1)} %copy-done.7, bf16[2,256,256]{2,1,0:T(8,128)(2,1)S(1)} %get-tuple-element.38.hats, bf16[4,256,256]{2,1,0:T(8,128)(2,1)S(1)} %get-tuple-element.39.invs, ...), custom_call_target="tpu_custom_call" | custom-call | flops 1073741824 | bytes 2097152 | tf_op jit(solution)/shard_map/sides/pallas_call | solution.py:519
  22.1 0.2 collective-permute-done.other_in
  22.3 4.6 %sweeps.1 = f32[2,256,256]{2,1,0:T(8,128)} custom-call(s32[1,1]{1,0:T(1,128)} %bitcast.14.wave, s32[1]{0:T(128)} %bitcast.1.own, f32[16,1,2560]{2,1,0:T(1,128)S(1)} %all-to-all-done.mine_in, f32[16,1,2560]{2,1,0:T(1,128)S(1)} %collective-permute-done.other_in, f32[4,32,32]{2,1,0:T(8,128)S(1)} %constant_dynamic-update-slice_fusion.coupling, ...), custom_call_target="tpu_custom_call" | custom-call | tf_op jit(solution)/shard_map/sweeps/pallas_call | solution.py:532
  (25 shorter events, 0.1 us)
Async XLA Ops:
  4.4 8.6 %copy-start.9 = (f32[4,4]{1,0:T(4,128)S(1)}, f32[4,4]{1,0:T(4,128)}, u32[]{:S(2)}) copy-start(f32[4,4]{1,0:T(4,128)} %param.14) | copy-start | bytes 196
  4.4 8.8 %copy-start.8 = (f32[8,8]{1,0:T(8,128)S(1)}, f32[8,8]{1,0:T(8,128)}, u32[]{:S(2)}) copy-start(f32[8,8]{1,0:T(8,128)} %param.15) | copy-start | bytes 772
  4.4 10.0 %copy-start.6 = (f32[256,256]{1,0:T(8,128)S(1)}, f32[256,256]{1,0:T(8,128)}, u32[]{:S(2)}) copy-start(f32[256,256]{1,0:T(8,128)} %mode.1) | copy-start | bytes 786436
  4.4 16.4 %all-to-all-start = ((f32[16,1,2560]{2,1,0:T(1,128)}), f32[16,1,2560]{2,1,0:T(1,128)S(1)}, u32[]{:S(2)}, u32[]{:S(2)}) async-start(f32[16,1,2560]{2,1,0:T(1,128)} %spectrum.1), calls=%async_computation | async-start | bytes 327680 | tf_op jit(solution)/shard_map/all_to_all | solution.py:494
  12.9 1.5 %copy-start.2 = (f32[2,256,256]{2,1,0:T(8,128)S(1)}, f32[2,256,256]{2,1,0:T(8,128)}, u32[]{:S(2)}) copy-start(f32[2,256,256]{2,1,0:T(8,128)} %forcing.1) | copy-start | bytes 1572868
  13.6 0.9 %copy-start.3 = (f32[256,1]{1,0:T(8,128)S(1)}, f32[256,1]{1,0:T(8,128)}, u32[]{:S(2)}) copy-start(f32[256,1]{1,0:T(8,128)} %constant.51.clone.lam_in.lam_col) | copy-start | bytes 3076
  13.8 1.0 %copy-start.1 = (bf16[256,256]{1,0:T(8,128)(2,1)S(1)}, bf16[256,256]{1,0:T(8,128)(2,1)}, u32[]{:S(2)}) copy-start(bf16[256,256]{1,0:T(8,128)(2,1)} %constant.48.clone.qh_in.qh) | copy-start | bytes 393220
  13.9 0.9 %copy-start = (bf16[256,256]{1,0:T(8,128)(2,1)S(1)}, bf16[256,256]{1,0:T(8,128)(2,1)}, u32[]{:S(2)}) copy-start(bf16[256,256]{1,0:T(8,128)(2,1)} %constant.49.clone.ql_in.ql) | copy-start | bytes 393220
  14.3 0.7 %copy-start.4 = (f32[8,256]{1,0:T(8,128)S(1)}, f32[8,256]{1,0:T(8,128)}, u32[]{:S(2)}) copy-start(f32[8,256]{1,0:T(8,128)} %constant.50.clone.rows_in.rows) | copy-start | bytes 24580
  14.4 0.7 %copy-start.5 = (s32[32]{0:T(128)S(1)}, s32[32]{0:T(128)}, u32[]{:S(2)}) copy-start(s32[32]{0:T(128)} %param.13) | copy-start | bytes 388
  15.1 5.8 %copy-start.7 = (f32[256,1]{1,0:T(8,128)S(1)}, f32[256,1]{1,0:T(8,128)}, u32[]{:S(2)}) copy-start(f32[256,1]{1,0:T(8,128)} %constant.52.clone.cols) | copy-start | bytes 3076
  20.9 1.4 %collective-permute-start = (f32[16,1,2560]{2,1,0:T(1,128)S(1)}, f32[16,1,2560]{2,1,0:T(1,128)S(1)}, u32[]{:S(2)}, u32[]{:S(2)}) collective-permute-start(f32[16,1,2560]{2,1,0:T(1,128)S(1)} %all-to-all-done.mine_in), channel_id=1, source_target_pairs={{0,8},{8,0},{16,24},{24,16},{1,9},{9,1},{17,25},{25,17},{2,10},{10... | collective-permute-start | bytes 491528 | tf_op jit(solution)/shard_map/ppermute | solution.py:518

commit v4 on v3

--- a/solution.py
+++ b/solution.py
@@ -35,7 +35,7 @@
     mul = functools.partial(lax.dot_general, dimension_numbers=dims, preferred_element_type=F32)
     (da,), (db,) = dims[0]
     size = ah.shape[1 - da]
-    if size <= 256 and da == 1 and size % 8 == 0:
+    if size <= 224 and da == 1 and size % 8 == 0:
         both = mul(jnp.concatenate([ah.astype(F32), al.astype(F32)], 0).astype(BF16), bh)
         return both[:size] + (both[size:] + mul(ah, bl))
     if ah.shape[da] % 128 == 0:
@@ -158,6 +158,21 @@
         out += [proj[0:1], proj[1:2]]
     flat = jnp.concatenate(out + vectors, 1)
     payload[...] = jnp.broadcast_to(flat[None], payload.shape)
+
+
+def spread(proj, side, ends, modes):
+    half, lane = 2 * modes, lanes((1, 4 * modes))
+    low = lane < half
+    if side in "tb":
+        real = jnp.where(low, proj, pltpu.roll(proj, half, 1))
+        imag = jnp.where(low, pltpu.roll(proj, half, 1), proj)
+    else:
+        by1, by2, by3 = (pltpu.roll(proj, k * modes, 1) for k in (1, 2, 3))
+        block = lane // modes
+        real = jnp.where(block == 0, proj, jnp.where(block == 3, by2, by1))
+        imag = jnp.where(block == 0, by2, jnp.where(block == 3, proj, by3))
+    parts = cmul((real, imag), ends[side])
+    return jnp.concatenate(parts, 1)
 
 
 def table_kernel(
@@ -183,7 +198,6 @@
         ],
         0,
     )
-    mode_out[0], mode_out[1] = split(mode[...])
 
     basis = (qh[...], ql[...])
     half_way = dot(forcing[...].reshape(2 * width, width), basis)
@@ -211,6 +225,11 @@
         er, ei, nr, ni = e[0], -e[1], n[0], -n[1]
         ends += [e[0], e[1], er - kappa * (ei - ni), ei + kappa * (er - nr)]
     ends_out[...] = jnp.concatenate(ends, 0)
+    met = {side: (ends[4 * k], ends[4 * k + 1]) for k, side in enumerate("btrl")}
+    shape = (4 * modes, 4 * modes)
+    eye = (lax.broadcasted_iota(jnp.int32, shape, 0) == lanes(shape)).astype(F32)
+    shares = jnp.concatenate([spread(eye, side, met, modes) for side in "tblr"], 0)
+    mode_out[0], mode_out[1] = split(dot(shares, mode[...], NT))
     line = lax.broadcasted_iota(jnp.int32, (width, 1), 0).astype(F32)
     phase = kappa * speeds[0] * line
     wave_out[0], wave_out[1] = jnp.cos(phase), jnp.sin(phase)
@@ -274,19 +293,6 @@
         ends[side] = (e[0], e[1]), (e[2], e[3])
     facing = {"t": "b", "b": "t", "l": "r", "r": "l"}
 
-    def spread(proj, side):
-        low = lane < half
-        if side in "tb":
-            real = jnp.where(low, proj, pltpu.roll(proj, half, 1))
-            imag = jnp.where(low, pltpu.roll(proj, half, 1), proj)
-        else:
-            by1, by2, by3 = (pltpu.roll(proj, k * modes, 1) for k in (1, 2, 3))
-            block = lane // modes
-            real = jnp.where(block == 0, proj, jnp.where(block == 3, by2, by1))
-            imag = jnp.where(block == 0, by2, jnp.where(block == 3, proj, by3))
-        parts = cmul((real, imag), ends[facing[side]][0])
-        return jnp.concatenate(parts, 1)
-
     def outgoing(c, side):
         z = cmul((c[:, : unknowns // 2], c[:, unknowns // 2 :]), ends[side][1])
         low = lane < half
@@ -310,10 +316,8 @@
         return [(out[2 * k * size : (2 * k + 1) * size], out[(2 * k + 1) * size : (2 * k + 2) * size]) for k in range(len(zs))]
 
     def coarse_of(weights, projs):
-        total = 0.0
-        for k, side in enumerate("tblr"):
-            total = total + spread(dot(weights[k], projs[side]), side)
-        return dot(total, mode_split, NT)
+        mixed = jnp.concatenate([dot(weights[k], projs[side]) for k, side in enumerate("tblr")], 1)
+        return dot(mixed, mode_split)
 
     def robin_of(c, base):
         tb = synth([outgoing(c, "t"), outgoing(c, "b")], along_hat)
@@ -411,10 +415,10 @@
     rowof = lambda z, k: (z[0][k : k + 1], z[1][k : k + 1])
 
     share, sent = project_sources(lambda o, src: out2[facing[src]]), project_sent(out2)
-    total = jnp.zeros((1, unknowns), F32)
-    for o in "tblr":
-        total = total + spread(base_proj[o][5:6] + share[o][index[o] : index[o] + 1] - sent[o][5:6], o)
-    c2 = dot(jnp.broadcast_to(total, (8, unknowns)), mode_split, NT)[0:1]
+    total = jnp.concatenate(
+        [base_proj[o][5:6] + share[o][index[o] : index[o] + 1] - sent[o][5:6] for o in "tblr"], 1
+    )
+    c2 = dot(jnp.broadcast_to(total, (8, 16 * modes)), mode_split)[0:1]
 
     mine_g = {s: rowof(out2[facing[s]], 4) for s in "tblr"}
     basis = (qh[...], ql[...])
@@ -500,7 +504,7 @@
             jax.ShapeDtypeStruct((4, width, width), BF16),
             jax.ShapeDtypeStruct((8, width), F32),
             jax.ShapeDtypeStruct((16, 4 * modes), F32),
-            jax.ShapeDtypeStruct((2, unknowns, unknowns), BF16),
+            jax.ShapeDtypeStruct((2, 16 * modes, unknowns), BF16),
             jax.ShapeDtypeStruct((2, width, 4 * modes), F32),
             jax.ShapeDtypeStruct((2, width, width), F32),
             jax.ShapeDtypeStruct((2, 8 * modes, width), BF16),

time: 27.2 us -> 26.8 us (0.985)
  waiting for transfers between devices: 3.01 us -> 1.5 us
  local copies, waits for them, and re-layouts: 1.72 us -> 2.67 us
  Pallas kernels: 12.5 us -> 12.8 us
    all_to_all x1, waiting for transfers between devices: 2.82 us -> 1.38 us  [local(): lax.all_to_all(payload, ('row', 'col'), 0, 0, axis_index_groups=groups, t...]
    unnamed x23, local copies, waits for them, and re-layouts: 0.73 us -> 1.68 us
    pallas_call x1, Pallas kernels: 2.9 us -> 3.39 us  [local(): pl.pallas_call(functools.partial(table_kernel, width=width, modes=modes),...]
  transfers between devices with their start and end apart: 2 -> 2, of which waited for: 2 -> 2; matrix products, arithmetic and copies ran while one was open for 5% -> 5% of each run, Pallas kernels for 15% -> 18%
where the time goes in v4:
time: 26.8 us; the launch traced here: 26.5 us
  Pallas kernels  12.8 us (48%)
  starting transfers between devices  8.36 us (31%)
  local copies, waits for them, and re-layouts  2.67 us (10%)
  waiting for transfers between devices  1.5 us (6%)
  between operations  0.85 us (3%)
  other arithmetic  0.35 us (1%)
    all_to_all x1, starting transfers between devices, local(): lax.all_to_all(payload, ('row', 'col'), 0, 0, axis_index_groups=groups, t...  8.35 us
    pallas_call x1, Pallas kernels, local(): pl.pallas_call(functools.partial(second_kernel, width=width, modes=modes,...  4.37 us
    pallas_call x1, Pallas kernels, local(): pl.pallas_call(functools.partial(first_kernel, width=width, modes=modes),...  3.74 us
    pallas_call x1, Pallas kernels, local(): pl.pallas_call(functools.partial(table_kernel, width=width, modes=modes),...  3.39 us
    unnamed x23, local copies, waits for them, and re-layouts  1.68 us
    all_to_all x1, waiting for transfers between devices, local(): lax.all_to_all(payload, ('row', 'col'), 0, 0, axis_index_groups=groups, t...  1.38 us
    pallas_call x1, Pallas kernels, local(): pl.pallas_call(functools.partial(side_kernel, width=width, modes=modes),...  1.27 us
  transfers between devices with their start and end apart: 2, of which 2 were waited for; matrix products, arithmetic and copies ran while one was open for 5% of the time, Pallas kernels for 18%

profile of v4, /device:TPU:0, one launch (start us, length us, event | category | flops | bytes accessed | tf_op | source)
XLA Modules:
  0.0 26.5 jit_solution(5328096905309909774)
XLA Ops:
  0.7 3.7 %spectrum.1 = f32[16,1,2560]{2,1,0:T(1,128)} custom-call(s32[1,1]{1,0:T(1,128)} %bitcast.12.wave_in, s32[1,32]{1,0:T(1,128)} %bitcast.15, f32[2,256,256]{2,1,0:T(8,128)} %forcing.1, bf16[256,256]{1,0:T(8,128)(2,1)} %constant.48.clone.qh_in.qh, bf16[256,256]{1,0:T(8,128)(2,1)} %constant.49.clone.ql_in.ql, f32[8,256]{1,0:T(8,128)} %constant.50.clone.rows_in.rows, ...), custom_call_target="tpu_custom_call" | custom-call | tf_op jit(solution)/shard_map/spectrum/pallas_call | solution.py:480
  4.4 0.0 copy-start.9
  4.4 0.0 copy-start.8
  4.4 8.4 %all-to-all-start = ((f32[16,1,2560]{2,1,0:T(1,128)}), f32[16,1,2560]{2,1,0:T(1,128)S(1)}, u32[]{:S(2)}, u32[]{:S(2)}) async-start(f32[16,1,2560]{2,1,0:T(1,128)} %spectrum.1), calls=%async_computation | async-start | bytes 327680 | tf_op jit(solution)/shard_map/all_to_all | solution.py:498
  12.9 0.1 fusion.3
  12.9 0.1 pad.32
  13.0 0.1 fusion.2
  13.1 0.1 pad.34
  13.2 0.1 broadcast_multiply_fusion
  13.3 0.1 mul.109
  13.4 0.1 mul.106
  13.5 0.0 copy-start.3
  13.5 0.1 broadcast_multiply_fusion.2
  13.6 0.1 mul.102
  13.7 0.1 mul.99
  13.9 0.1 fusion.1
  13.9 0.1 fusion
  14.0 0.1 pad.45.clone
  14.1 0.1 pad_bitcast_fusion
  14.2 0.1 select_bitcast_fusion
  14.2 0.2 copy-done.3
  14.4 0.2 copy-done.1
  14.6 0.1 copy-done
  14.7 0.2 copy-done.4
  14.9 0.0 copy-done.5
  14.9 0.9 %copy-done.6 = f32[256,256]{1,0:T(8,128)S(1)} copy-done((f32[256,256]{1,0:T(8,128)S(1)}, f32[256,256]{1,0:T(8,128)}, u32[]{:S(2)}) %copy-start.6) | copy-done | bytes 262168
  15.9 3.4 %tables.1 = (bf16[4,256,256]{2,1,0:T(8,128)(2,1)S(1)}, f32[8,256]{1,0:T(8,128)S(1)}, f32[16,128]{1,0:T(8,128)S(1)}, bf16[2,512,256]{2,1,0:T(8,128)(2,1)S(1)}, f3...) custom-call(s32[1,1]{1,0:T(1,128)} %bitcast.13.wave, ...), custom_call_target="tpu_custom_call" | custom-call | flops 1073741824 | bytes 2097152 | tf_op jit(solution)/shard_map/tables/pallas_call | solution.py:501
  19.3 0.1 maximum_maximum_fusion.picks
  19.3 1.4 %all-to-all-done.mine_in = f32[16,1,2560]{2,1,0:T(1,128)S(1)} async-done(((f32[16,1,2560]{2,1,0:T(1,128)}), f32[16,1,2560]{2,1,0:T(1,128)S(1)}, u32[]{:S(2)}, u32[]{:S(2)}) %all-to-all-start) | async-done | bytes 163872 | tf_op jit(solution)/shard_map/all_to_all | solution.py:498
  20.7 1.3 %sides.1 = (bf16[2,1024,256]{2,1,0:T(8,128)(2,1)S(1)}, f32[4,256,256]{2,1,0:T(8,128)S(1)}, bf16[2,256,256]{2,1,0:T(8,128)(2,1)S(1)}) custom-call(f32[8,256]{1,0:T(8,128)S(1)} %copy-done.4, f32[256,1]{1,0:T(8,128)S(1)} %copy-done.7, bf16[2,256,256]{2,1,0:T(8,128)(2,1)S(1)} %get-tuple-element.38.hats, bf16[4,256,256]{2,1,0:T(8,128)(2,1)S(1)} %get-tuple-element.39.invs, ...), custom_call_target="tpu_custom_call" | custom-call | flops 1073741824 | bytes 2097152 | tf_op jit(solution)/shard_map/sides/pallas_call | solution.py:523
  22.0 0.1 collective-permute-done.other_in
  22.1 4.4 %sweeps.1 = f32[2,256,256]{2,1,0:T(8,128)} custom-call(s32[1,1]{1,0:T(1,128)} %bitcast.14.wave, s32[1]{0:T(128)} %bitcast.1.own, f32[16,1,2560]{2,1,0:T(1,128)S(1)} %all-to-all-done.mine_in, f32[16,1,2560]{2,1,0:T(1,128)S(1)} %collective-permute-done.other_in, f32[4,32,32]{2,1,0:T(8,128)S(1)} %constant_dynamic-update-slice_fusion.coupling, ...), custom_call_target="tpu_custom_call" | custom-call | tf_op jit(solution)/shard_map/sweeps/pallas_call | solution.py:536
  (25 shorter events, 0.1 us)
Async XLA Ops:
  4.4 8.4 %copy-start.9 = (f32[4,4]{1,0:T(4,128)S(1)}, f32[4,4]{1,0:T(4,128)}, u32[]{:S(2)}) copy-start(f32[4,4]{1,0:T(4,128)} %param.14) | copy-start | bytes 196
  4.4 8.6 %copy-start.8 = (f32[8,8]{1,0:T(8,128)S(1)}, f32[8,8]{1,0:T(8,128)}, u32[]{:S(2)}) copy-start(f32[8,8]{1,0:T(8,128)} %param.15) | copy-start | bytes 772
  4.4 16.3 %all-to-all-start = ((f32[16,1,2560]{2,1,0:T(1,128)}), f32[16,1,2560]{2,1,0:T(1,128)S(1)}, u32[]{:S(2)}, u32[]{:S(2)}) async-start(f32[16,1,2560]{2,1,0:T(1,128)} %spectrum.1), calls=%async_computation | async-start | bytes 327680 | tf_op jit(solution)/shard_map/all_to_all | solution.py:498
  12.8 1.5 %copy-start.2 = (f32[2,256,256]{2,1,0:T(8,128)S(1)}, f32[2,256,256]{2,1,0:T(8,128)}, u32[]{:S(2)}) copy-start(f32[2,256,256]{2,1,0:T(8,128)} %forcing.1) | copy-start | bytes 1572868
  13.5 0.9 %copy-start.3 = (f32[256,1]{1,0:T(8,128)S(1)}, f32[256,1]{1,0:T(8,128)}, u32[]{:S(2)}) copy-start(f32[256,1]{1,0:T(8,128)} %constant.51.clone.lam_in.lam_col) | copy-start | bytes 3076
  13.7 1.0 %copy-start.1 = (bf16[256,256]{1,0:T(8,128)(2,1)S(1)}, bf16[256,256]{1,0:T(8,128)(2,1)}, u32[]{:S(2)}) copy-start(bf16[256,256]{1,0:T(8,128)(2,1)} %constant.48.clone.qh_in.qh) | copy-start | bytes 393220
  13.8 0.9 %copy-start = (bf16[256,256]{1,0:T(8,128)(2,1)S(1)}, bf16[256,256]{1,0:T(8,128)(2,1)}, u32[]{:S(2)}) copy-start(bf16[256,256]{1,0:T(8,128)(2,1)} %constant.49.clone.ql_in.ql) | copy-start | bytes 393220
  14.2 0.7 %copy-start.4 = (f32[8,256]{1,0:T(8,128)S(1)}, f32[8,256]{1,0:T(8,128)}, u32[]{:S(2)}) copy-start(f32[8,256]{1,0:T(8,128)} %constant.50.clone.rows_in.rows) | copy-start | bytes 24580
  14.2 0.7 %copy-start.5 = (s32[32]{0:T(128)S(1)}, s32[32]{0:T(128)}, u32[]{:S(2)}) copy-start(s32[32]{0:T(128)} %param.13) | copy-start | bytes 388
  14.9 0.9 %copy-start.6 = (f32[256,256]{1,0:T(8,128)S(1)}, f32[256,256]{1,0:T(8,128)}, u32[]{:S(2)}) copy-start(f32[256,256]{1,0:T(8,128)} %mode.1) | copy-start | bytes 786436
  15.9 4.9 %copy-start.7 = (f32[256,1]{1,0:T(8,128)S(1)}, f32[256,1]{1,0:T(8,128)}, u32[]{:S(2)}) copy-start(f32[256,1]{1,0:T(8,128)} %constant.52.clone.cols) | copy-start | bytes 3076
  20.7 1.4 %collective-permute-start = (f32[16,1,2560]{2,1,0:T(1,128)S(1)}, f32[16,1,2560]{2,1,0:T(1,128)S(1)}, u32[]{:S(2)}, u32[]{:S(2)}) collective-permute-start(f32[16,1,2560]{2,1,0:T(1,128)S(1)} %all-to-all-done.mine_in), channel_id=1, source_target_pairs={{0,8},{8,0},{16,24},{24,16},{1,9},{9,1},{17,25},{25,17},{2,10},{10... | collective-permute-start | bytes 491528 | tf_op jit(solution)/shard_map/ppermute | solution.py:522
